TPU v7x, 256 devices: a whole 4x4x8 slice. The times are simulated.
256 devices in a mesh: gx: 8 (over x, core), gy: 8 (over z), wa: 4 (over y).
Axes of the slice: x: 4, y: 4, z: 8, core: 2. Of those that a mesh axis runs over, the one named last changes fastest.
Arguments:
- velocity: float32 [3, 256, 512, 512], P(None, 'gx', 'gy', 'wa'), may hold values from -70 to 70, as said below
- lengths: int32 [8, 8, 4, 2048], P('gx', 'gy', 'wa'), may hold values from 16 to 128
- destinations: int32 [8, 8, 4, 2048, 1], P('gx', 'gy', 'wa'), may hold values from 0 to 63; in each aligned block of 2048 rows (0 to 2047, 2048 to 4095, ..., all dimensions but the last counted through in order) at most 64 rows name the same one
Outputs:
- received: float32 [64, 4, 3, 64, 64, 128], P(('gx', 'gy'), 'wa')
Inputs may be any that keep to these rules, and one draw needn't show every extreme that they name: `velocity`: finite values; the amplitude varies over the grid. `destinations`: in every draw no device sends more than 64 blocks to one writer, and some device sends exactly 64 to one writer.
All inputs are finite; a program needn't handle non-finite values.
Results may differ from a plain program's by a relative error of at most 0.0003.
Values sent between devices are 32-bit elements; how exact they have to be, the bound alone decides.
No kernel may reach another device: no remote copies, remote signals or barrier semaphores. Data moves between devices by JAX's collectives and lax.ppermute only.
A program may use at most 128 MiB of HBM per device.

v0:
```python
import jax
import jax.numpy as jnp
from jax import lax
from jax.sharding import Mesh
from jax.sharding import PartitionSpec as P

BY = 8
BZ = 16
GX_GY_WA = ("gx_0", "gx_1", "gy", "wa")
GX = ("gx_0", "gx_1")
GX_GY = ("gx_0", "gx_1", "gy")


def extended(array, sides, width):
    for axis, dim in sides:
        peers, length = (lax.axis_size(axis), array.shape[dim])
        up = [(i, (i + 1) % peers) for i in range(peers)]
        down = [(j, i) for i, j in up]
        last = lax.slice_in_dim(array, length - width, length, axis=dim)
        leading = lax.slice_in_dim(array, 0, width, axis=dim)
        before = lax.ppermute(last, axis, up)
        after = lax.ppermute(leading, axis, down)
        array = jnp.concatenate([before, array, after], axis=dim)
    return array


def over_axes(array, axes):
    for axis in axes:
        array = lax.psum(array, axis)
    return array


def dct_table(count):
    freqs = jnp.arange(count, dtype=jnp.float32)[:, None]
    points = jnp.arange(count, dtype=jnp.float32)[None, :]
    table = jnp.cos(jnp.pi * (points + 0.5) * freqs / count) * jnp.sqrt(2.0 / count)
    return jnp.where(freqs == 0.0, table * jnp.sqrt(0.5), table)


def curl_field(padded):

    def along_x(component):
        return (padded[component, 2:, 1:-1, 1:-1] - padded[component, :-2, 1:-1, 1:-1]) * 0.5

    def along_y(component):
        return (padded[component, 1:-1, 2:, 1:-1] - padded[component, 1:-1, :-2, 1:-1]) * 0.5

    def along_z(component):
        return (padded[component, 1:-1, 1:-1, 2:] - padded[component, 1:-1, 1:-1, :-2]) * 0.5

    first = along_y(2) - along_z(1)
    second = along_z(0) - along_x(2)
    third = along_x(1) - along_y(0)
    return jnp.stack([first, second, third])


def transform(curl):
    comps, cells_x, cells_y, cells_z = curl.shape
    kron_table = jnp.kron(dct_table(BY), dct_table(BZ)).T.reshape(BY, BZ, BY * BZ)
    grouped = curl.reshape(comps, cells_x, cells_y // BY, BY, cells_z // BZ, BZ)
    coeffs = lax.dot_general(
        grouped,
        kron_table,
        (((3, 5), (0, 1)), ((), ())),
        precision=lax.Precision.HIGHEST,
        preferred_element_type=jnp.float32,
    )
    return coeffs.reshape(comps, -1, BY * BZ)


def local(velocity, lengths, destinations):
    padded = extended(velocity, ((GX, 1), ("gy", 2), ("wa", 3)), 1)
    curl = curl_field(padded)
    coeffs = transform(curl)
    total = over_axes(jnp.sum(coeffs * coeffs), GX_GY_WA)
    every = curl.size * lax.axis_size(GX) * lax.axis_size("gy") * lax.axis_size("wa")
    rms = jnp.sqrt(total / every + 1e-06)
    comps, nblk, width = coeffs.shape
    rows_x = lax.axis_size(GX)
    rows_y = lax.axis_size("gy")
    writer_count = rows_x * rows_y
    capacity = max(2, 2 * nblk // writer_count)
    targets = destinations.reshape(nblk)
    lens = lengths.reshape(nblk)
    onehot = (targets[:, None] == jnp.arange(writer_count, dtype=jnp.int32)[None, :]).astype(
        jnp.int32
    )
    before = jnp.cumsum(onehot, axis=0) - onehot
    ranking = jnp.sum(before * onehot, axis=1)
    slot_index = targets * capacity + ranking
    source = jnp.full((writer_count * capacity,), -1, jnp.int32)
    source = source.at[slot_index].set(jnp.arange(nblk, dtype=jnp.int32))
    present = source >= 0
    safe = jnp.maximum(source, 0)
    picked = jnp.take(coeffs, safe, axis=1)
    freqs = jnp.arange(width, dtype=jnp.int32)
    keep = (freqs[None, :] < jnp.take(lens, safe)[:, None]) & present[:, None]
    outgoing = jnp.where(keep[None, :, :], picked / rms, 0.0)
    outgoing = outgoing.reshape(comps, writer_count, capacity, width)
    arrived = lax.all_to_all(outgoing, GX_GY, split_axis=1, concat_axis=1, tiled=True)
    return arrived.reshape(1, 1, comps, writer_count, capacity, width)


def solution(mesh):
    finer = Mesh(
        mesh.devices.reshape(4, 2, mesh.shape["gy"], mesh.shape["wa"]), ("gx_0", "gx_1", "gy", "wa")
    )
    return jax.shard_map(
        local,
        mesh=finer,
        in_specs=(P(None, GX, "gy", "wa"), P(GX, "gy", "wa", None), P(GX, "gy", "wa", None, None)),
        out_specs=P(GX_GY, "wa", None, None, None, None),
        check_vma=False,
    )
```

profile of v0, /device:TPU:1, one launch (start us, length us, event | category | flops | bytes accessed | tf_op | source)
XLA Modules:
  0.0 446.5 jit_solution(11419711120034385909)
XLA Ops:
  0.0 0.0 copy-start
  0.0 1.0 fusion.18
  1.0 2.6 collective-permute-start
  3.6 0.6 collective-permute-start.1
  4.3 0.7 fusion.11
  5.0 18.1 %reduce-window.6 = s32[64,16,128]{2,1,0:T(8,128)S(1)} reduce-window(s32[64,16,128]{2,1,0:T(8,128)S(1)} %fusion.11, s32[]{:T(128)} %constant.25.clone.1), window={size=1x1x128 pad=0_0x0_0x127_0}, to_apply=%region_0.1 | reduce-window | flops 16646144 | bytes 1048580 | tf_op jit(solution)/shard_map/reduce-window
  23.1 0.2 slice.96
  23.4 0.4 copy.38
  23.8 0.2 reduce-window.9
  24.0 0.2 broadcast_add_fusion
  24.2 0.0 copy-done.7
  24.2 0.3 fusion.10
  24.5 8.1 %scatter_custom_fusion = s32[4096]{0:T(1024)S(1)} fusion(s32[2048]{0:T(1024)S(1)} %bitcast.68, s32[2048]{0:T(1024)S(1)} %iota.50, s32[]{:T(128)} %constant.22.clone.1), kind=kCustom, calls=%fused_computation.48 | custom fusion | bytes 16388 | tf_op jit(solution)/shard_map/scatter | solution.py:92
  32.6 23.0 %gather_fusion = s32[4096]{0:T(1024)S(1)} fusion(s32[2048]{0:T(1024)S(1)} %bitcast.54, s32[4096]{0:T(1024)S(1)} %maximum_clamp_fusion), kind=kCustom, calls=%fused_computation | custom fusion | bytes 49152 | tf_op jit(solution)/shard_map/jit(_take)/gather | solution.py:97
  55.7 0.1 lt.43
  55.7 0.1 and.19
  55.8 0.1 multiply_select_fusion
  55.9 0.1 multiply_select_fusion.1
  56.0 2.3 fusion.7
  58.4 0.1 broadcast_multiply_fusion
  58.5 0.2 mul.189
  58.7 0.0 collective-permute-done
  58.7 0.9 constant_dynamic-update-slice_fusion.6
  59.6 2.8 constant_dynamic-update-slice_fusion.5
  62.4 0.0 collective-permute-done.1
  62.5 0.9 constant_dynamic-update-slice_fusion.3
  63.4 0.7 fusion.15
  64.1 5.0 %collective-permute-start.2 = (f32[3,34,1,128]{3,2,1,0:T(1,128)}, f32[3,34,1,128]{3,2,1,0:T(1,128)S(1)}, u32[]{:S(2)}, u32[]{:S(2)}) collective-permute-start(f32[3,34,1,128]{3,2,1,0:T(1,128)} %get-tuple-element.18), channel_id=1, source_target_pairs={{4,0},{8,4},{12,8},{16,12},{20,16},{24,20},{28,24},{0,28},{5,1},{9... | collective-permute-start | bytes 156680 | tf_op jit(solution)/shard_map/ppermute | solution.py:22
  69.0 0.0 collective-permute-start.3
  69.0 1.5 fusion.17
  70.6 1.5 fusion.16
  72.0 3.6 copy.41
  75.6 3.7 copy.42
  79.3 3.7 copy.43
  83.0 3.8 copy.44
  86.8 0.0 collective-permute-done.2
  86.8 0.0 collective-permute-done.3
  86.8 2.5 pad_maximum_fusion.2
  89.3 10.2 %copy.23 = f32[3,34,66,128]{1,3,2,0:T(8,128)} copy(f32[3,34,66,128]{3,2,1,0:T(8,128)} %pad_maximum_fusion.2) | data formatting | bytes 6893568 | tf_op jit(solution)/shard_map/concatenate | solution.py:23
  99.4 2.2 fusion.14
  101.7 2.7 collective-permute-start.4
  104.4 0.0 collective-permute-start.5
  104.4 2.3 pad_maximum_fusion.5
  106.7 3.8 copy.45
  110.4 2.7 copy.46
  113.1 10.3 %multiply_subtract_fusion = f32[1,32,64,128]{1,3,2,0:T(8,128)} fusion(f32[1,32,64,128]{1,3,2,0:T(8,128)} %copy.45, f32[1,32,64,128]{1,3,2,0:T(8,128)} %copy.46, f32[1,32,64,128]{1,3,2,0:T(8,128)} %copy.43, f32[1,32,64,128]{1,3,2,0:T(8,128)} %copy.44), kind=kLoop, calls=%fused_computation.15 | loop fusion | flops 1310720 | bytes 5242880 | tf_op jit(solution)/shard_map/sub | solution.py:53
  123.4 2.7 copy.39
  126.2 2.8 copy.40
  129.0 0.0 collective-permute-done.4
  129.0 0.0 collective-permute-done.5
  129.0 18.5 %fusion.6 = (f32[1,32,64,128]{1,3,2,0:T(8,128)}, f32[1,32,64,128]{1,3,2,0:T(8,128)}) fusion(f32[3,34,66,128]{1,3,2,0:T(8,128)} %copy.23, f32[3,34,66,1]{1,3,2,0:T(1,128)} %collective-permute-done.5, f32[3,34,66,1]{1,3,2,0:T(1,128)} %collective-permute-done.4, f32[1,32,64,128]{1,3,2,0:T(8,128)} %copy.39, f32[1,32,64,128]{1,3,2,0:T(8,128)} %copy.40, ...), kind=kLoop, calls=%fused_computation.14 | loop fusion | flops 3670016 | bytes 9792096 | tf_op jit(solution)/shard_map/sub | solution.py:51
  147.5 10.3 %maximum_bitcast_fusion = f32[3,32,8,8,8,16]{1,5,3,4,2,0:T(8,128)} fusion(f32[1,32,8,8,8,16]{1,5,4,3,2,0:T(8,128)S(1)} %bitcast.58, f32[1,32,8,8,8,16]{1,5,4,3,2,0:T(8,128)} %bitcast.60, f32[1,32,8,8,8,16]{1,5,4,3,2,0:T(8,128)} %bitcast.59), kind=kLoop, calls=%fused_computation.3 | loop fusion | flops 1572864 | bytes 6291456 | tf_op jit(solution)/shard_map/dot_general | solution.py:61
  157.8 23.1 %copy.47 = f32[3,32,8,8,8,16]{5,3,2,1,4,0:T(8,128)} copy(f32[3,32,8,8,8,16]{1,5,3,4,2,0:T(8,128)} %maximum_bitcast_fusion) | data formatting | bytes 6291456 | tf_op jit(solution)/shard_map/dot_general | solution.py:61
  180.9 24.0 %multiply_reduce_fusion = (f32[]{:T(128)}, f32[3,2048,128]{2,1,0:T(8,128)S(1)}) fusion(f32[3,2048,8,16]{3,1,2,0:T(8,128)} %bitcast.55, f32[8,16,128,1]{2,1,0,3:T(8,128)S(1)} %bitcast.62), kind=kOutput, calls=%fused_computation.17 | convolution fusion | flops 1209532416 | bytes 6356996 | tf_op jit(solution)/shard_map/dot_general | solution.py:61
  204.9 8.1 %psum.28 = f32[]{:T(128)} all-reduce(f32[]{:T(128)} %get-tuple-element.32), channel_id=1, replica_groups=mesh['gx_0'=4,'gx_1'=2,'gy'=8,'wa'=4] {'gx_0'}, use_global_device_ids=true, to_apply=%region_5.6 | all-reduce | flops 1 | bytes 8 | tf_op jit(solution)/shard_map/psum | solution.py:29
  212.9 0.1 broadcast_in_dim.69
  213.0 7.0 %psum.29 = f32[]{:T(128)} all-reduce(f32[]{:T(128)} %psum.28), channel_id=1, replica_groups=mesh['gx_0'=4,'gx_1'=2,'gy'=8,'wa'=4] {'gx_1'}, use_global_device_ids=true, to_apply=%region_6.7 | all-reduce | flops 1 | bytes 8 | tf_op jit(solution)/shard_map/psum | solution.py:29
  220.0 10.0 %copy.34 = f32[3,2048,128]{2,0,1:T(4,128)} copy(f32[3,2048,128]{2,1,0:T(8,128)S(1)} %get-tuple-element.33) | data formatting | bytes 6291456 | tf_op jit(solution)/shard_map/dot_general | solution.py:61
  229.9 14.2 %psum.30 = f32[]{:T(128)} all-reduce(f32[]{:T(128)} %psum.29), channel_id=1, replica_groups=mesh['gx_0'=4,'gx_1'=2,'gy'=8,'wa'=4] {'gy'}, use_global_device_ids=true, to_apply=%region_7.8 | all-reduce | flops 1 | bytes 8 | tf_op jit(solution)/shard_map/psum | solution.py:29
  244.2 32.5 %gather_fusion.1 = f32[4096,3,128]{2,1,0:T(4,128)} fusion(f32[3,2048,128]{2,0,1:T(4,128)} %copy.34, s32[4096]{0:T(1024)S(1)} %maximum_clamp_fusion), kind=kCustom, calls=%fused_computation.1 | custom fusion | bytes 12599296 | tf_op jit(solution)/shard_map/jit(_take)/gather | solution.py:95
  276.7 9.5 %psum.31 = f32[]{:T(128)} all-reduce(f32[]{:T(128)} %psum.30), channel_id=1, replica_groups=mesh['gx_0'=4,'gx_1'=2,'gy'=8,'wa'=4] {'wa'}, use_global_device_ids=true, to_apply=%region_8.9 | all-reduce | flops 1 | bytes 8 | tf_op jit(solution)/shard_map/psum | solution.py:29
  286.9 5.0 %fusion.1 = f32[3,64,64,128]{3,2,0,1:T(8,128)S(1)} fusion(f32[3,64,64,128]{3,0,2,1:T(4,128)} %bitcast.56, f32[]{:T(128)S(6)} %sqrt.3, pred[64,64]{1,0:T(8,128)(4,1)S(1)} %broadcast_in_dim.69, pred[64,64,128]{2,1,0:T(8,128)(4,1)S(1)} %copy-done.6), kind=kLoop, calls=%fused_computation.6 | loop fusion | flops 4718592 | bytes 13111300 | tf_op jit(solution)/shard_map/jit(_where)/select_n | solution.py:98
  291.9 151.2 %all_to_all.5 = f32[3,64,64,128]{3,2,0,1:T(8,128)S(1)} all-to-all(f32[3,64,64,128]{3,2,0,1:T(8,128)S(1)} %fusion.1), channel_id=1, replica_groups=mesh['gx_0'=4,'gx_1'=2,'gy'=8,'wa'=4] {'gx_0','gx_1','gy'}, dimensions={1} | all-to-all | bytes 12582912 | tf_op jit(solution)/shard_map/all_to_all | solution.py:100
  443.2 3.3 copy.36
  (23 shorter events, 0.1 us)
Async XLA Ops:
  0.0 32.6 %copy-start = (s32[1,1,1,2048]{3,2,1,0:T(1,128)S(1)}, s32[1,1,1,2048]{3,2,1,0:T(1,128)}, u32[]{:S(2)}) copy-start(s32[1,1,1,2048]{3,2,1,0:T(1,128)} %param.4) | copy-start | bytes 24580
  0.0 24.2 %copy-start.7 = (s32[1,1,1,2048,1]{3,4,2,1,0:T(1,128)S(1)}, s32[1,1,1,2048,1]{3,4,2,1,0:T(1,128)}, u32[]{:S(2)}) copy-start(s32[1,1,1,2048,1]{3,4,2,1,0:T(1,128)} %param.5) | copy-start | bytes 24580
  1.0 57.7 %collective-permute-start = (f32[3,1,64,128]{3,2,1,0:T(8,128)S(1)}, f32[3,1,64,128]{3,2,1,0:T(8,128)}, u32[]{:S(2)}, u32[]{:S(2)}) collective-permute-start(f32[3,1,64,128]{3,2,1,0:T(8,128)S(1)} %get-tuple-element.27), channel_id=1, source_target_pairs={{0,32},{32,64},{64,96},{96,128},{128,160},{160,192},{192,224},{224... | collective-permute-start | bytes 294920 | tf_op jit(solution)/shard_map/ppermute | solution.py:21
  3.6 58.9 %collective-permute-start.1 = (f32[3,1,64,128]{3,2,1,0:T(8,128)S(1)}, f32[3,1,64,128]{3,2,1,0:T(8,128)}, u32[]{:S(2)}, u32[]{:S(2)}) collective-permute-start(f32[3,1,64,128]{3,2,1,0:T(8,128)S(1)} %get-tuple-element.26), channel_id=1, source_target_pairs={{32,0},{64,32},{96,64},{128,96},{160,128},{192,160},{224,192},{0,2... | collective-permute-start | bytes 294920 | tf_op jit(solution)/shard_map/ppermute | solution.py:22
  64.1 22.7 %collective-permute-start.2 = (f32[3,34,1,128]{3,2,1,0:T(1,128)}, f32[3,34,1,128]{3,2,1,0:T(1,128)S(1)}, u32[]{:S(2)}, u32[]{:S(2)}) collective-permute-start(f32[3,34,1,128]{3,2,1,0:T(1,128)} %get-tuple-element.18), channel_id=1, source_target_pairs={{4,0},{8,4},{12,8},{16,12},{20,16},{24,20},{28,24},{0,28},{5,1},{9... | collective-permute-start | bytes 156680 | tf_op jit(solution)/shard_map/ppermute | solution.py:22
  69.0 17.8 %collective-permute-start.3 = (f32[3,34,1,128]{3,2,1,0:T(1,128)}, f32[3,34,1,128]{3,2,1,0:T(1,128)S(1)}, u32[]{:S(2)}, u32[]{:S(2)}) collective-permute-start(f32[3,34,1,128]{3,2,1,0:T(1,128)} %get-tuple-element.17), channel_id=1, source_target_pairs={{0,4},{4,8},{8,12},{12,16},{16,20},{20,24},{24,28},{28,0},{1,5},{5... | collective-permute-start | bytes 156680 | tf_op jit(solution)/shard_map/ppermute | solution.py:21
  101.7 27.3 %collective-permute-start.4 = (f32[3,34,66,1]{1,3,2,0:T(1,128)}, f32[3,34,66,1]{1,3,2,0:T(1,128)}, u32[]{:S(2)}, u32[]{:S(2)}) collective-permute-start(f32[3,34,66,1]{1,3,2,0:T(1,128)} %get-tuple-element.9), channel_id=1, source_target_pairs={{1,0},{2,1},{3,2},{0,3},{5,4},{6,5},{7,6},{4,7},{9,8},{10,9},{11,1... | collective-permute-start | bytes 80792 | tf_op jit(solution)/shard_map/ppermute | solution.py:22
  104.4 24.6 %collective-permute-start.5 = (f32[3,34,66,1]{1,3,2,0:T(1,128)}, f32[3,34,66,1]{1,3,2,0:T(1,128)}, u32[]{:S(2)}, u32[]{:S(2)}) collective-permute-start(f32[3,34,66,1]{1,3,2,0:T(1,128)} %get-tuple-element.10), channel_id=1, source_target_pairs={{0,1},{1,2},{2,3},{3,0},{4,5},{5,6},{6,7},{7,4},{8,9},{9,10},{10,1... | collective-permute-start | bytes 80792 | tf_op jit(solution)/shard_map/ppermute | solution.py:21
  106.7 3.8 copy-start.5
  113.1 10.3 %copy-start.4 = (f32[1,32,64,128]{3,2,1,0:T(8,128)S(1)}, f32[1,32,64,128]{3,2,1,0:T(8,128)}, u32[]{:S(2)}) copy-start(f32[1,32,64,128]{3,2,1,0:T(8,128)} %get-tuple-element.16) | copy-start | bytes 3145732
  123.4 2.7 copy-start.3
  129.0 18.5 %copy-start.2 = (f32[1,32,64,128]{1,3,2,0:T(8,128)S(1)}, f32[1,32,64,128]{1,3,2,0:T(8,128)}, u32[]{:S(2)}) copy-start(f32[1,32,64,128]{1,3,2,0:T(8,128)} %multiply_subtract_fusion) | copy-start | bytes 3145732
  244.2 42.7 %copy-start.6 = (pred[64,64,128]{2,1,0:T(8,128)(4,1)S(1)}, pred[64,64,128]{2,1,0:T(8,128)(4,1)}, u32[]{:S(2)}) copy-start(pred[64,64,128]{2,1,0:T(8,128)(4,1)} %fusion.7) | copy-start | bytes 1572868
  443.2 3.3 copy-start.1
where the time goes:
time: 448 us; the launch traced here: 446 us
  blocking collectives  190 us (42%)
  local copies, waits for them, and re-layouts  149 us (33%)
  other arithmetic  71.2 us (16%)
  matrix products  24 us (5%)
  starting transfers between devices  10.9 us (2%)
    all_to_all x1, blocking collectives, local(): lax.all_to_all(outgoing, GX_GY, split_axis=1, concat_axis=1, tiled=True)  151 us
    psum x4, blocking collectives, over_axes(): array = lax.psum(array, axis)  38.8 us
    dot_general x2, local copies, waits for them, and re-layouts, transform(): lax.dot_general(grouped, kron_table, (((3, 5), (0, 1)), ((), ())), precis...  33 us
    gather x1, local copies, waits for them, and re-layouts, local(): picked = jnp.take(coeffs, safe, axis=1)  32.5 us
    unnamed x25, local copies, waits for them, and re-layouts  27.7 us
    dot_general x1, matrix products, transform(): lax.dot_general(grouped, kron_table, (((3, 5), (0, 1)), ((), ())), precis...  24 us
    gather x1, local copies, waits for them, and re-layouts, local(): keep = (freqs[None, :] < jnp.take(lens, safe)[:, None]) & present[:, None]  23 us
    another operation x3, other arithmetic  18.5 us
  transfers between devices with their start and end apart: 6, of which 0 were waited for; matrix products, arithmetic and copies ran while one was open for 22% of the time, Pallas kernels for 0%

commit v1 on v0

v1 whole, which is shorter than its diff:
```python
import functools

import jax
import jax.numpy as jnp
import numpy as np
from jax import lax
from jax.experimental import pallas as pl
from jax.experimental.pallas import tpu as pltpu
from jax.sharding import PartitionSpec as P

BY = 8
BZ = 16
LANES = 128
COMP = 3
CX = 32
CY = 64
NBLK = 2048
WRITERS = 64
CAP = 64
ROWS = 45
CELLS = 256 * 512 * 512 * 3
G = ("gx", "gy")


def span_of(rows):
    return -(-(COMP * rows + 1) // 8) * 8


def dct_np(n):
    k = np.arange(n, dtype=np.float64)[:, None]
    j = np.arange(n, dtype=np.float64)[None, :]
    t = np.sqrt(2.0 / n) * np.cos(np.pi * (j + 0.5) * k / n)
    t[0] *= np.sqrt(0.5)
    return t


def table_np():
    k = (0.5 * np.kron(dct_np(BY), dct_np(BZ)).T).astype(np.float32)
    high = k.astype(jnp.bfloat16)
    low = (k - high.astype(np.float32)).astype(jnp.bfloat16)
    top = np.concatenate([high, low], axis=1)
    bottom = np.concatenate([high, np.zeros_like(low)], axis=1)
    return np.concatenate([top, bottom], axis=0)


def iota(shape, dim):
    return lax.broadcasted_iota(jnp.int32, shape, dim)


def faces_kernel(vel, xlo, xhi, ylo, yhi, zt):
    plane = CY
    comp = CX * CY
    for n, c in enumerate((1, 2)):
        xlo[n * plane : (n + 1) * plane] = vel[c * comp : c * comp + plane]
        xhi[n * plane : (n + 1) * plane] = vel[(c + 1) * comp - plane : (c + 1) * comp]
    for n, c in enumerate((0, 2)):
        ylo[n * CX : (n + 1) * CX] = vel[pl.ds(c * comp, CX, stride=plane)]
        yhi[n * CX : (n + 1) * CX] = vel[pl.ds(c * comp + plane - 1, CX, stride=plane)]
    lane = iota((CY, LANES), 1)
    t = jnp.zeros((CY, LANES), jnp.float32)
    for k in range(2 * CX):
        f = vel[k * plane : (k + 1) * plane]
        t = jnp.where((lane >> 1) == k, pltpu.roll(f, (2 * k + 1) % LANES, 1), t)
    zt[...] = t


def faces(vel2):
    f32 = jnp.float32
    return pl.pallas_call(
        faces_kernel,
        out_shape=[
            jax.ShapeDtypeStruct((2 * CY, LANES), f32),
            jax.ShapeDtypeStruct((2 * CY, LANES), f32),
            jax.ShapeDtypeStruct((2 * CX, LANES), f32),
            jax.ShapeDtypeStruct((2 * CX, LANES), f32),
            jax.ShapeDtypeStruct((CY, LANES), f32),
        ],
        cost_estimate=pl.CostEstimate(flops=4_000_000, bytes_accessed=3_500_000, transcendentals=0),
        name="faces",
    )(vel2)


def index_kernel(tgt, length, words, wide, head):
    chunks = NBLK // LANES
    t = tgt[...]
    ln = length[...]
    row = iota((WRITERS, LANES), 0)
    before = (iota((LANES, LANES), 0) < iota((LANES, LANES), 1)).astype(jnp.bfloat16)
    ones = jnp.ones((LANES, LANES), jnp.bfloat16)
    rhs = jnp.concatenate([before, ones], axis=1)
    hits, weighted = [], []
    for r in range(chunks):
        hit = t[r : r + 1, :] == row
        hits.append(hit)
        weighted.append(jnp.where(hit, ln[r : r + 1, :], 0).astype(jnp.float32).astype(jnp.bfloat16))
    counted = [jnp.where(h, 1.0, 0.0).astype(jnp.bfloat16) for h in hits]
    nt = (((1,), (1,)), ((), ()))
    base_l = jnp.zeros((WRITERS, LANES), jnp.float32)
    base_c = jnp.zeros((WRITERS, LANES), jnp.float32)
    lens = jnp.zeros((WRITERS, LANES), jnp.float32)
    starts = []
    for r in range(chunks):
        sums_l = jnp.dot(weighted[r], rhs, preferred_element_type=jnp.float32)
        sums_c = jnp.dot(counted[r], rhs, preferred_element_type=jnp.float32)
        start = jnp.where(hits[r], sums_l[:, :LANES] + base_l, 0.0)
        rank = jnp.where(hits[r], sums_c[:, :LANES] + base_c, 0.0)
        starts.append(jnp.sum(start, axis=0, keepdims=True))
        slot = jnp.sum(rank, axis=0, keepdims=True).astype(jnp.int32)
        at = jnp.where(slot == iota((LANES, LANES), 0), 1.0, 0.0).astype(jnp.bfloat16)
        lens += lax.dot_general(weighted[r], at, nt, preferred_element_type=jnp.float32)
        base_l += sums_l[:, LANES:]
        base_c += sums_c[:, LANES:]
    start = jnp.concatenate(starts, axis=0).astype(jnp.int32)
    first = start >> 7
    shift = start & (LANES - 1)
    over = jnp.maximum(shift + ln - LANES, 0)
    for out, rows in ((words, ROWS), (wide, CAP)):
        addr = t * span_of(rows) + COMP * jnp.minimum(first, rows - 1)
        lo = jnp.where(first < rows, shift, LANES)
        second = jnp.where(first + 1 < rows, over, 0)
        out[...] = addr + (lo << 14) + (second << 22)
    full = jnp.max(base_l, axis=0, keepdims=True)
    spill = jnp.where(full > ROWS * LANES, 1.0, 0.0)
    lane = iota((WRITERS, LANES), 1)
    head[...] = jnp.where(lane < CAP, lens, jnp.where(lane == CAP + 1, spill, 0.0))


def index(targets, lens):
    i32 = jnp.int32
    return pl.pallas_call(
        index_kernel,
        out_shape=[
            jax.ShapeDtypeStruct((NBLK // LANES, LANES), i32),
            jax.ShapeDtypeStruct((NBLK // LANES, LANES), i32),
            jax.ShapeDtypeStruct((WRITERS, LANES), jnp.float32),
        ],
        cost_estimate=pl.CostEstimate(flops=20_000_000, bytes_accessed=100_000, transcendentals=0),
        name="index",
    )(targets, lens)


PLANES = 4


def transform_kernel(vel, xprev, xnext, yprev, ynext, zprev, znext, table, out, sq, ends, scratch, blocks):
    step = pl.program_id(0)
    comp = CX * CY
    lane = iota((CY, LANES), 1)
    row = iota((CY, LANES), 0)

    @pl.when(step == 0)
    def _():
        ends[...] = jnp.where(
            (lane & 1) == 0, pltpu.roll(znext[...], LANES - 1, 1), pltpu.roll(zprev[...], 1, 1)
        )
        sq[...] = jnp.zeros_like(sq)

    first, last = lane == 0, lane == LANES - 1
    granule = iota((8, LANES), 1) >> 4

    def plane_of(c, x):
        return vel[pl.ds(pl.multiple_of(c * comp + x * CY, CY), CY)]

    def along_x(c, x, n):
        low = jnp.maximum(x - 1, 0)
        high = jnp.minimum(x + 1, CX - 1)
        below = jnp.where(x == 0, xprev[n * CY : (n + 1) * CY], plane_of(c, low))
        above = jnp.where(x == CX - 1, xnext[n * CY : (n + 1) * CY], plane_of(c, high))
        return above - below

    def along_y(f, x, n):
        above = jnp.where(row == CY - 1, ynext[pl.ds(n * CX + x, CY, stride=0)], pltpu.roll(f, CY - 1, 0))
        below = jnp.where(row == 0, yprev[pl.ds(n * CX + x, CY, stride=0)], pltpu.roll(f, 1, 0))
        return above - below

    def along_z(f, c, x):
        edge = pltpu.roll(ends[...], LANES - 1 - 2 * (c * CX + x), 1)
        above = jnp.where(last, edge, pltpu.roll(f, LANES - 1, 1))
        below = jnp.where(first, edge, pltpu.roll(f, 1, 1))
        return above - below

    total = jnp.zeros((8, LANES), jnp.float32)
    for p in range(PLANES):
        x = step * PLANES + p
        u, v, w = plane_of(0, x), plane_of(1, x), plane_of(2, x)
        curl = (
            along_y(w, x, 1) - along_z(v, 1, x),
            along_z(u, 0, x) - along_x(2, x, 1),
            along_x(1, x, 0) - along_y(u, x, 0),
        )
        for c in range(COMP):
            f = curl[c]
            square = f * f
            for i in range(CY // 8):
                total += square[i * 8 : (i + 1) * 8]
            at = (p * COMP + c) * CY
            scratch[at : at + CY] = f
            tiles = [scratch[pl.ds(at + y, 8, stride=8)] for y in range(8)]
            for b in (4, 2, 1):
                low = (granule & b) == 0
                fresh = list(tiles)
                for j in range(8):
                    if j & b == 0:
                        one, two = tiles[j], tiles[j | b]
                        fresh[j] = jnp.where(low, one, pltpu.roll(two, 16 * b, 1))
                        fresh[j | b] = jnp.where(low, pltpu.roll(one, LANES - 16 * b, 1), two)
                tiles = fresh
            whole = jnp.concatenate(tiles, axis=0)
            high = whole.astype(jnp.bfloat16)
            low = (whole - high.astype(jnp.float32)).astype(jnp.bfloat16)
            blocks[at : at + CY, :LANES] = high
            blocks[at : at + CY, LANES:] = low
    sq[...] += total
    for p in range(PLANES):
        at = p * COMP * CY
        both = jnp.dot(
            blocks[at : at + COMP * CY], table[...], preferred_element_type=jnp.float32
        )
        coeffs = both[:, :LANES] + both[:, LANES:]
        for c in range(COMP):
            for zb in range(8):
                piece = coeffs[c * CY + zb * 8 : c * CY + zb * 8 + 8]
                out[pl.ds(COMP * (p * CY + zb * 8) + c, 8, stride=COMP)] = piece


def transform(vel2, xprev, xnext, yprev, ynext, zprev, znext):
    table = jnp.asarray(table_np())
    rows = PLANES * COMP * CY
    whole = lambda a: pl.BlockSpec(a.shape, lambda i: (0, 0))
    args = (vel2, xprev, xnext, yprev, ynext, zprev, znext, table)
    return pl.pallas_call(
        transform_kernel,
        grid=(CX // PLANES,),
        in_specs=[whole(a) for a in args],
        out_specs=[
            pl.BlockSpec((rows, LANES), lambda i: (i, 0)),
            pl.BlockSpec((8, LANES), lambda i: (0, 0)),
        ],
        out_shape=[
            jax.ShapeDtypeStruct((COMP * NBLK, LANES), jnp.float32),
            jax.ShapeDtypeStruct((8, LANES), jnp.float32),
        ],
        scratch_shapes=[
            pltpu.VMEM((CY, LANES), jnp.float32),
            pltpu.VMEM((rows, LANES), jnp.float32),
            pltpu.VMEM((rows, 2 * LANES), jnp.bfloat16),
        ],
        cost_estimate=pl.CostEstimate(
            flops=2 * COMP * NBLK * 256 * 256, bytes_accessed=6_500_000, transcendentals=0
        ),
        name="transform",
    )(*args)


PACK_STEPS = 4


def pack_kernel(limit, words, coeffs, out):
    step = pl.program_id(0)
    per = NBLK // LANES // PACK_STEPS
    lane = iota((COMP, LANES), 1)

    def body(r, carry):
        at = step * per + r
        for j in range(LANES):
            plane, yb, zb = j // CY, (j % CY) // 8, j % 8
            word = words[at, j]
            addr = word & 16383
            lo = (word >> 14) & 255
            second = word >> 22
            source = COMP * (plane * CY + zb * 8 + yb)
            value = coeffs[pl.ds(r * (COMP * LANES) + source, COMP)]
            turned = pltpu.roll(value, lo & (LANES - 1), 1)
            pltpu.store(out.at[pl.ds(addr, COMP)], turned, mask=lane >= lo)
            nxt = jnp.minimum(addr + COMP, limit)
            pltpu.store(out.at[pl.ds(nxt, COMP)], turned, mask=lane < second)
        return carry

    lax.fori_loop(0, per, body, 0)


def pack(words, coeffs, rows):
    span = span_of(rows)
    block = COMP * NBLK // PACK_STEPS
    return pl.pallas_call(
        functools.partial(pack_kernel, WRITERS * span - COMP),
        grid=(PACK_STEPS,),
        in_specs=[
            pl.BlockSpec(memory_space=pltpu.SMEM),
            pl.BlockSpec((block, LANES), lambda i: (i, 0)),
        ],
        out_specs=pl.BlockSpec((WRITERS * span, LANES), lambda i: (0, 0)),
        out_shape=jax.ShapeDtypeStruct((WRITERS * span, LANES), jnp.float32),
        cost_estimate=pl.CostEstimate(
            flops=200_000_000, bytes_accessed=8_000_000, transcendentals=0
        ),
        name=f"pack{rows}",
    )(words, coeffs)


def decode_kernel(head, words, scale, spill):
    h = head[...]
    lane = iota((WRITERS, LANES), 1)
    lens = jnp.where(lane < CAP, h, 0.0)
    before = (iota((LANES, LANES), 0) < iota((LANES, LANES), 1)).astype(jnp.bfloat16)
    start = jnp.dot(lens.astype(jnp.bfloat16), before, preferred_element_type=jnp.float32)
    start = start.astype(jnp.int32)
    words[...] = (
        COMP * (start >> 7) + ((start & (LANES - 1)) << 8) + (lens.astype(jnp.int32) << 16)
    )
    total = jnp.sum(jnp.where(lane == CAP, h, 0.0), keepdims=True)
    rms = jnp.sqrt(total * (1.0 / CELLS) + 1e-6)
    scale[...] = jnp.broadcast_to(1.0 / rms, scale.shape)
    flag = jnp.max(jnp.where(lane == CAP + 1, h, 0.0), keepdims=True)
    spill[...] = jnp.broadcast_to(flag, spill.shape).astype(jnp.int32)


def decode(head):
    return pl.pallas_call(
        decode_kernel,
        out_shape=[
            jax.ShapeDtypeStruct((WRITERS, LANES), jnp.int32),
            jax.ShapeDtypeStruct((8, LANES), jnp.float32),
            jax.ShapeDtypeStruct((8, LANES), jnp.int32),
        ],
        name="decode",
    )(head)


SOURCES = 8


def unpack_kernel(span, words, scale, recv, out):
    step = pl.program_id(0)
    lane = iota((COMP, LANES), 1)
    factor = scale[0:COMP, :]
    flat = out.reshape(COMP * SOURCES * CAP, LANES)
    limit = SOURCES * span - COMP

    def body(s, carry):
        base = s * span
        for q in range(CAP):
            word = words[step * SOURCES + s, q]
            lo = (word >> 8) & 255
            count = word >> 16
            at = jnp.minimum(base + (word & 255), limit)
            one = recv[pl.ds(at, COMP)]
            two = recv[pl.ds(jnp.minimum(at + COMP, limit), COMP)]
            both = jnp.where(lane >= lo, one, two)
            turned = pltpu.roll(both, (LANES - lo) & (LANES - 1), 1)
            value = jnp.where(lane < count, turned * factor, 0.0)
            flat[pl.ds(s * CAP + q, COMP, stride=SOURCES * CAP)] = value
        return carry

    lax.fori_loop(0, SOURCES, body, 0)


def unpack(words, scale, recv, rows):
    span = span_of(rows)
    return pl.pallas_call(
        functools.partial(unpack_kernel, span),
        grid=(WRITERS // SOURCES,),
        in_specs=[
            pl.BlockSpec(memory_space=pltpu.SMEM),
            pl.BlockSpec((8, LANES), lambda i: (0, 0)),
            pl.BlockSpec((SOURCES * span, LANES), lambda i: (i, 0)),
        ],
        out_specs=pl.BlockSpec((COMP, SOURCES * CAP, LANES), lambda i: (0, i, 0)),
        out_shape=jax.ShapeDtypeStruct((COMP, WRITERS * CAP, LANES), jnp.float32),
        cost_estimate=pl.CostEstimate(
            flops=200_000_000, bytes_accessed=11_000_000, transcendentals=0
        ),
        name=f"unpack{rows}",
    )(words, scale, recv)


def exchange(buffer, rows):
    span = span_of(rows)
    got = lax.all_to_all(buffer.reshape(WRITERS, span, LANES), G, 0, 0, tiled=True)
    return got


def local(velocity, lengths, destinations):
    vel2 = velocity.reshape(COMP * CX * CY, LANES)
    targets = destinations.reshape(NBLK // LANES, LANES)
    lens = lengths.reshape(NBLK // LANES, LANES)

    xlo, xhi, ylo, yhi, zt = faces(vel2)

    def ring(axis, n, d):
        return functools.partial(
            lax.ppermute, axis_name=axis, perm=[(i, (i + d) % n) for i in range(n)]
        )

    n_x, n_y, n_z = (lax.axis_size(a) for a in ("gx", "gy", "wa"))
    xprev, xnext = ring("gx", n_x, 1)(xhi), ring("gx", n_x, -1)(xlo)
    yprev, ynext = ring("gy", n_y, 1)(yhi), ring("gy", n_y, -1)(ylo)
    zprev, znext = ring("wa", n_z, 1)(zt), ring("wa", n_z, -1)(zt)
    words, wide, head = index(targets, lens)

    coeffs, sq = transform(vel2, xprev, xnext, yprev, ynext, zprev, znext)

    lane = lax.broadcasted_iota(jnp.int32, (1, LANES), 1)
    mine = jnp.where(lane == CAP, 0.25 * jnp.sum(sq), jnp.where(lane == CAP + 1, head[0:1], 0.0))
    for b in (1, 2):
        other = lax.ppermute(mine, "wa", [(i, i ^ b) for i in range(n_z)])
        mine = jnp.where(lane == CAP, mine + other, jnp.maximum(mine, other))
    packed = pack(words, coeffs, ROWS).reshape(WRITERS, span_of(ROWS), LANES)
    full_head = jnp.where(lane < CAP, head, mine)[:, None, :]
    packed = lax.dynamic_update_slice(packed, full_head, (0, COMP * ROWS, 0))

    got = exchange(packed, ROWS)
    inner, scale, spill = decode(got[:, COMP * ROWS, :])

    def usual(_):
        return unpack(inner, scale, got.reshape(-1, LANES), ROWS)

    def wider(_):
        again = exchange(pack(wide, coeffs, CAP), CAP)
        return unpack(inner, scale, again.reshape(-1, LANES), CAP)

    out = lax.cond(spill[0, 0] > 0, wider, usual, None)
    return out.reshape(1, 1, COMP, WRITERS, CAP, LANES)


def solution(mesh):
    return jax.shard_map(
        local,
        mesh=mesh,
        in_specs=(
            P(None, "gx", "gy", "wa"),
            P("gx", "gy", "wa", None),
            P("gx", "gy", "wa", None, None),
        ),
        out_specs=P(G, "wa", None, None, None, None),
        check_vma=False,
    )
```

time: 448 us -> 197 us (0.44)
  local copies, waits for them, and re-layouts: 149 us -> 6.84 us
  blocking collectives: 190 us -> 114 us
  other arithmetic: 71.2 us -> 2.66 us
  Pallas kernels: 0 us -> 55.8 us
  matrix products: 24 us -> 0 us
    pallas_call x0 -> x6, Pallas kernels: none -> 55.8 us  [the longest x1 24.9 us: unpack(): pl.pallas_call(functools.partial(unpack_kernel, span), grid=(WRITERS // S...]
    gather x2 -> x0, local copies, waits for them, and re-layouts: 55.5 us -> none  [the longest x1 32.5 us: local(): picked = jnp.take(coeffs, safe, axis=1)]
    psum x4 -> x0, blocking collectives: 38.8 us -> none  [over_axes(): array = lax.psum(array, axis)]
    all_to_all x1, blocking collectives: 151 us -> 114 us  [exchange(): lax.all_to_all(buffer.reshape(WRITERS, span, LANES), G, 0, 0, tiled=True)]
    dot_general x2 -> x0, local copies, waits for them, and re-layouts: 33 us -> none  [transform(): lax.dot_general(grouped, kron_table, (((3, 5), (0, 1)), ((), ())), precis...]
    sub x2 -> x0, other arithmetic: 28.8 us -> none  [the longest x1 18.5 us: curl_field(): first = along_y(2) - along_z(1)]
    unnamed x25 -> x16, local copies, waits for them, and re-layouts: 27.7 us -> 3.26 us
    dot_general x1 -> x0, matrix products: 24 us -> none  [transform(): lax.dot_general(grouped, kron_table, (((3, 5), (0, 1)), ((), ())), precis...]
  transfers between devices with their start and end apart: 6 -> 8, of which waited for: 0 -> 2; matrix products, arithmetic and copies ran while one was open for 22% -> 0% of each run, Pallas kernels for 0% -> 8%
where the time goes in v1:
time: 197 us; the launch traced here: 196 us
  blocking collectives  114 us (58%)
  Pallas kernels  55.8 us (28%)
  starting transfers between devices  11.3 us (6%)
  local copies, waits for them, and re-layouts  6.84 us (3%)
  waiting for transfers between devices  4.4 us (2%)
  other arithmetic  2.66 us (1%)
    all_to_all x1, blocking collectives, exchange(): lax.all_to_all(buffer.reshape(WRITERS, span, LANES), G, 0, 0, tiled=True)  114 us
    pallas_call x1, Pallas kernels, unpack(): pl.pallas_call(functools.partial(unpack_kernel, span), grid=(WRITERS // S...  24.9 us
    pallas_call x1, Pallas kernels, pack(): pl.pallas_call(functools.partial(pack_kernel, WRITERS * span - COMP), gri...  13.8 us
    pallas_call x1, Pallas kernels, transform(): pl.pallas_call(transform_kernel, grid=(CX // PLANES,), in_specs=[whole(a)...  10.3 us
    ppermute x2, starting transfers between devices, local(): yprev, ynext = (ring('gy', n_y, 1)(yhi), ring('gy', n_y, -1)(ylo))  6.12 us
  transfers between devices with their start and end apart: 8, of which 2 were waited for; matrix products, arithmetic and copies ran while one was open for 0% of the time, Pallas kernels for 8%

profile of v1, /device:TPU:1, one launch (start us, length us, event | category | flops | bytes accessed | tf_op | source)
XLA Modules:
  0.0 196.2 jit_solution(15555911489275289609)
XLA Ops:
  0.0 3.1 %faces.1 = (f32[128,128]{1,0:T(8,128)}, f32[128,128]{1,0:T(8,128)}, f32[64,128]{1,0:T(8,128)}, f32[64,128]{1,0:T(8,128)}, f32[64,128]{1,0:T(8,128)}) custom-call(f32[6144,128]{1,0:T(8,128)} %bitcast.22), custom_call_target="tpu_custom_call" | custom-call | flops 4000000 | bytes 3500000 | tf_op jit(solution)/shard_map/faces/pallas_call | solution.py:69
  3.1 2.5 %collective-permute-start.2 = (f32[64,128]{1,0:T(8,128)}, f32[64,128]{1,0:T(8,128)S(1)}, u32[]{:S(2)}, u32[]{:S(2)}) collective-permute-start(f32[64,128]{1,0:T(8,128)} %get-tuple-element.46), channel_id=1, source_target_pairs={{0,4},{4,8},{8,12},{12,16},{16,20},{20,24},{24,28},{28,0},{1,5},{5... | collective-permute-start | bytes 98312 | tf_op jit(solution)/shard_map/ppermute | solution.py:397
  5.6 2.1 %collective-permute-start = (f32[128,128]{1,0:T(8,128)}, f32[128,128]{1,0:T(8,128)S(1)}, u32[]{:S(2)}, u32[]{:S(2)}) collective-permute-start(f32[128,128]{1,0:T(8,128)} %get-tuple-element.44), channel_id=1, source_target_pairs={{0,32},{32,64},{64,96},{96,128},{128,160},{160,192},{192,224},{224... | collective-permute-start | bytes 196616 | tf_op jit(solution)/shard_map/ppermute | solution.py:396
  7.6 0.0 collective-permute-start.1
  7.6 3.7 %collective-permute-start.3 = (f32[64,128]{1,0:T(8,128)}, f32[64,128]{1,0:T(8,128)S(1)}, u32[]{:S(2)}, u32[]{:S(2)}) collective-permute-start(f32[64,128]{1,0:T(8,128)} %get-tuple-element.47), channel_id=1, source_target_pairs={{0,28},{4,0},{8,4},{12,8},{16,12},{20,16},{24,20},{28,24},{1,29},{... | collective-permute-start | bytes 98312 | tf_op jit(solution)/shard_map/ppermute | solution.py:397
  11.3 2.7 %collective-permute-start.5 = (f32[64,128]{1,0:T(8,128)}, f32[64,128]{1,0:T(8,128)S(1)}, u32[]{:S(2)}, u32[]{:S(2)}) collective-permute-start(f32[64,128]{1,0:T(8,128)} %get-tuple-element.48), channel_id=1, source_target_pairs={{0,3},{1,0},{2,1},{3,2},{4,7},{5,4},{6,5},{7,6},{8,11},{9,8},{10,9... | collective-permute-start | bytes 98312 | tf_op jit(solution)/shard_map/ppermute | solution.py:398
  14.0 0.0 collective-permute-done.2.yprev
  14.0 0.0 copy-start.4
  14.0 0.0 collective-permute-start.4
  14.0 2.2 %index.1 = (s32[16,128]{1,0:T(8,128)}, s32[16,128]{1,0:T(8,128)S(1)}, f32[64,128]{1,0:T(8,128)}) custom-call(s32[16,128]{1,0:T(8,128)} %bitcast.28, s32[16,128]{1,0:T(8,128)} %bitcast.29), custom_call_target="tpu_custom_call" | custom-call | flops 20000000 | bytes 100000 | tf_op jit(solution)/shard_map/index/pallas_call | solution.py:130
  16.2 0.0 copy-start.3
  16.2 0.0 collective-permute-done.3.ynext
  16.2 0.0 copy-start.5
  16.2 0.0 collective-permute-done.5.znext
  16.2 0.0 copy-start.6
  16.2 2.0 %collective-permute-done.4.zprev = f32[64,128]{1,0:T(8,128)S(1)} collective-permute-done((f32[64,128]{1,0:T(8,128)}, f32[64,128]{1,0:T(8,128)S(1)}, u32[]{:S(2)}, u32[]{:S(2)}) %collective-permute-start.4) | collective-permute-done | bytes 32800 | tf_op jit(solution)/shard_map/ppermute | solution.py:398
  18.2 0.0 copy-start.7
  18.2 0.0 collective-permute-done.xprev
  18.2 0.0 copy-start.1
  18.2 0.0 collective-permute-done.1.xnext
  18.2 0.0 copy-done.4
  18.2 0.0 copy-done.5
  18.2 0.0 copy-done.6
  18.3 0.6 copy-done.7
  18.8 0.0 copy-done.1
  18.9 0.0 copy-start.2
  18.9 0.6 copy-done.2
  19.5 10.3 %transform.1 = (f32[6144,128]{1,0:T(8,128)S(1)}, f32[8,128]{1,0:T(8,128)}) custom-call(f32[6144,128]{1,0:T(8,128)} %bitcast.23, f32[128,128]{1,0:T(8,128)} %copy-done.1, f32[128,128]{1,0:T(8,128)} %copy-done.2, f32[64,128]{1,0:T(8,128)} %copy-done.4, f32[64,128]{1,0:T(8,128)} %copy-done.5, f32[64,128]{1,0:T(8,128)} %copy-done.7, f32[64,128]{1,0:T(8,128)} %copy-done.6, ...), custom_call_target="tpu_custom_call" | custom-call | flops 805306368 | bytes 6500000 | tf_op jit(solution)/shard_map/transform/pallas_call | solution.py:231
  29.8 1.3 reduce_sum.9
  31.7 0.7 fusion
  32.4 0.0 collective-permute-start.6
  32.4 2.4 %collective-permute-done.6 = f32[1,128]{1,0:T(1,128)S(1)} collective-permute-done((f32[1,128]{1,0:T(1,128)S(1)}, f32[1,128]{1,0:T(1,128)S(1)}, u32[]{:S(2)}, u32[]{:S(2)}) %collective-permute-start.6) | collective-permute-done | bytes 544 | tf_op jit(solution)/shard_map/ppermute | solution.py:406
  34.8 0.7 maximum_select_fusion
  35.5 0.4 collective-permute-start.7
  35.9 13.8 %pack45.1 = f32[8704,128]{1,0:T(8,128)} custom-call(s32[16,128]{1,0:T(8,128)} %get-tuple-element.43.words, f32[6144,128]{1,0:T(8,128)S(1)} %get-tuple-element.49.coeffs), custom_call_target="tpu_custom_call" | custom-call | flops 200000000 | bytes 8000000 | tf_op jit(solution)/shard_map/pack45/pallas_call | solution.py:285
  49.7 0.0 collective-permute-done.7
  49.7 0.0 copy-done.3
  49.7 1.7 dynamic_update_slice.3
  51.5 113.8 %all_to_all.10 = f32[64,136,128]{2,1,0:T(8,128)S(1)} all-to-all(f32[64,136,128]{2,1,0:T(8,128)} %dynamic_update_slice.3), channel_id=1, replica_groups=mesh['gx'=8,'gy'=8,'wa'=4] {'gx','gy'}, dimensions={0} | all-to-all | bytes 8912896 | tf_op jit(solution)/shard_map/all_to_all | solution.py:379
  165.3 0.0 copy-start
  165.3 2.0 %copy-done = f32[64,136,128]{2,1,0:T(8,128)} copy-done((f32[64,136,128]{2,1,0:T(8,128)}, f32[64,136,128]{2,1,0:T(8,128)S(1)}, u32[]{:S(2)}) %copy-start) | copy-done | bytes 4456472
  167.3 0.6 slice.12
  168.0 1.5 decode.1
  169.5 1.2 slice.11
  171.3 24.9 %conditional.1 = (f32[1,1,3,64,64,128]{5,4,3,2,1,0:T(8,128)}) conditional(s32[]{:T(128)} %bitcast.13, (f32[64,136,128]{2,1,0:T(8,128)}, s32[64,128]{1,0:T(8,128)S(1)}, f32[8,128]{1,0:T(8,128)S(1)}) %tuple.21, (s32[16,128]{1,0:T(8,128)S(1)}, f32[6144,128]{1,0:T(8,128)S(1)}, s32[64,128]{1,0:T(8,128)S(1)}, f32[8,128]{1,0:T(8,128)S(1)}) %tuple.14), branch_computations={%region_1.2_spmd, %region_2.3_spmd} | conditional | flops 400000000 | bytes 32107208 | solution.py:422
  171.3 24.9 %unpack45.1 = f32[3,4096,128]{2,1,0:T(8,128)} custom-call(s32[64,128]{1,0:T(8,128)S(1)} %get-tuple-element.23.words, f32[8,128]{1,0:T(8,128)S(1)} %get-tuple-element.24.scale, f32[8704,128]{1,0:T(8,128)} %bitcast.20), custom_call_target="tpu_custom_call" | custom-call | flops 200000000 | bytes 11000000 | tf_op jit(solution)/shard_map/cond/branch_0_fun/unpack45/pallas_call | solution.py:360
  (3 shorter events, 0.0 us)
Async XLA Ops:
  3.1 10.9 %collective-permute-start.2 = (f32[64,128]{1,0:T(8,128)}, f32[64,128]{1,0:T(8,128)S(1)}, u32[]{:S(2)}, u32[]{:S(2)}) collective-permute-start(f32[64,128]{1,0:T(8,128)} %get-tuple-element.46), channel_id=1, source_target_pairs={{0,4},{4,8},{8,12},{12,16},{16,20},{20,24},{24,28},{28,0},{1,5},{5... | collective-permute-start | bytes 98312 | tf_op jit(solution)/shard_map/ppermute | solution.py:397
  5.6 12.6 %collective-permute-start = (f32[128,128]{1,0:T(8,128)}, f32[128,128]{1,0:T(8,128)S(1)}, u32[]{:S(2)}, u32[]{:S(2)}) collective-permute-start(f32[128,128]{1,0:T(8,128)} %get-tuple-element.44), channel_id=1, source_target_pairs={{0,32},{32,64},{64,96},{96,128},{128,160},{160,192},{192,224},{224... | collective-permute-start | bytes 196616 | tf_op jit(solution)/shard_map/ppermute | solution.py:396
  7.6 10.6 %collective-permute-start.1 = (f32[128,128]{1,0:T(8,128)}, f32[128,128]{1,0:T(8,128)S(1)}, u32[]{:S(2)}, u32[]{:S(2)}) collective-permute-start(f32[128,128]{1,0:T(8,128)} %get-tuple-element.45), channel_id=1, source_target_pairs={{0,224},{32,0},{64,32},{96,64},{128,96},{160,128},{192,160},{224,1... | collective-permute-start | bytes 196616 | tf_op jit(solution)/shard_map/ppermute | solution.py:396
  7.6 8.6 %collective-permute-start.3 = (f32[64,128]{1,0:T(8,128)}, f32[64,128]{1,0:T(8,128)S(1)}, u32[]{:S(2)}, u32[]{:S(2)}) collective-permute-start(f32[64,128]{1,0:T(8,128)} %get-tuple-element.47), channel_id=1, source_target_pairs={{0,28},{4,0},{8,4},{12,8},{16,12},{20,16},{24,20},{28,24},{1,29},{... | collective-permute-start | bytes 98312 | tf_op jit(solution)/shard_map/ppermute | solution.py:397
  11.3 4.9 %collective-permute-start.5 = (f32[64,128]{1,0:T(8,128)}, f32[64,128]{1,0:T(8,128)S(1)}, u32[]{:S(2)}, u32[]{:S(2)}) collective-permute-start(f32[64,128]{1,0:T(8,128)} %get-tuple-element.48), channel_id=1, source_target_pairs={{0,3},{1,0},{2,1},{3,2},{4,7},{5,4},{6,5},{7,6},{8,11},{9,8},{10,9... | collective-permute-start | bytes 98312 | tf_op jit(solution)/shard_map/ppermute | solution.py:398
  14.0 4.2 %copy-start.4 = (f32[64,128]{1,0:T(8,128)}, f32[64,128]{1,0:T(8,128)S(1)}, u32[]{:S(2)}) copy-start(f32[64,128]{1,0:T(8,128)S(1)} %collective-permute-done.2.yprev) | copy-start | bytes 98308
  14.0 4.2 %collective-permute-start.4 = (f32[64,128]{1,0:T(8,128)}, f32[64,128]{1,0:T(8,128)S(1)}, u32[]{:S(2)}, u32[]{:S(2)}) collective-permute-start(f32[64,128]{1,0:T(8,128)} %get-tuple-element.48), channel_id=1, source_target_pairs={{0,1},{1,2},{2,3},{3,0},{4,5},{5,6},{6,7},{7,4},{8,9},{9,10},{10,1... | collective-permute-start | bytes 98312 | tf_op jit(solution)/shard_map/ppermute | solution.py:398
  16.2 33.5 %copy-start.3 = (f32[64,128]{1,0:T(8,128)S(1)}, f32[64,128]{1,0:T(8,128)}, u32[]{:S(2)}) copy-start(f32[64,128]{1,0:T(8,128)} %get-tuple-element.50) | copy-start | bytes 98308
  16.2 2.0 %copy-start.5 = (f32[64,128]{1,0:T(8,128)}, f32[64,128]{1,0:T(8,128)S(1)}, u32[]{:S(2)}) copy-start(f32[64,128]{1,0:T(8,128)S(1)} %collective-permute-done.3.ynext) | copy-start | bytes 98308
  16.2 2.0 %copy-start.6 = (f32[64,128]{1,0:T(8,128)}, f32[64,128]{1,0:T(8,128)S(1)}, u32[]{:S(2)}) copy-start(f32[64,128]{1,0:T(8,128)S(1)} %collective-permute-done.5.znext) | copy-start | bytes 98308
  18.2 0.6 copy-start.7
  18.2 0.6 copy-start.1
  18.9 0.6 copy-start.2
  32.4 2.4 %collective-permute-start.6 = (f32[1,128]{1,0:T(1,128)S(1)}, f32[1,128]{1,0:T(1,128)S(1)}, u32[]{:S(2)}, u32[]{:S(2)}) collective-permute-start(f32[1,128]{1,0:T(1,128)S(1)} %fusion), channel_id=1, source_target_pairs={{0,1},{1,0},{2,3},{3,2},{4,5},{5,4},{6,7},{7,6},{8,9},{9,8},{10,11... | collective-permute-start | bytes 1544 | tf_op jit(solution)/shard_map/ppermute | solution.py:406
  35.5 14.2 %collective-permute-start.7 = (f32[1,128]{1,0:T(1,128)S(1)}, f32[1,128]{1,0:T(1,128)S(1)}, u32[]{:S(2)}, u32[]{:S(2)}) collective-permute-start(f32[1,128]{1,0:T(1,128)S(1)} %maximum_select_fusion), channel_id=1, source_target_pairs={{0,2},{1,3},{2,0},{3,1},{4,6},{5,7},{6,4},{7,5},{8,10},{9,11},{10,... | collective-permute-start | bytes 1544 | tf_op jit(solution)/shard_map/ppermute | solution.py:406
  165.3 2.0 %copy-start = (f32[64,136,128]{2,1,0:T(8,128)}, f32[64,136,128]{2,1,0:T(8,128)S(1)}, u32[]{:S(2)}) copy-start(f32[64,136,128]{2,1,0:T(8,128)S(1)} %all_to_all.10) | copy-start | bytes 13369348

commit v2 on v1

v2 whole, which is shorter than its diff:
```python
import functools

import jax
import jax.numpy as jnp
import numpy as np
from jax import lax
from jax.experimental import pallas as pl
from jax.experimental.pallas import tpu as pltpu
from jax.sharding import PartitionSpec as P

BY = 8
BZ = 16
LANES = 128
COMP = 3
CX = 32
CY = 64
NBLK = 2048
WRITERS = 64
CAP = 64
ROWS = 45
CELLS = 256 * 512 * 512 * 3
G = ("gx", "gy")


def span_of(rows):
    return -(-(COMP * rows + 1) // 8) * 8


def room_of(rows):
    return -(-(COMP * rows + 6) // 8) * 8


def dct_np(n):
    k = np.arange(n, dtype=np.float64)[:, None]
    j = np.arange(n, dtype=np.float64)[None, :]
    t = np.sqrt(2.0 / n) * np.cos(np.pi * (j + 0.5) * k / n)
    t[0] *= np.sqrt(0.5)
    return t


def tables_np():
    k = (0.5 * np.kron(dct_np(BY), dct_np(BZ)).T).astype(np.float32)
    high = k.astype(jnp.bfloat16)
    low = (k - high.astype(np.float32)).astype(jnp.bfloat16)
    top = np.concatenate([high, low], axis=1)
    bottom = np.concatenate([high, np.zeros_like(low)], axis=1)
    turned = [np.concatenate([np.roll(part, BZ * zb, axis=0) for part in (top, bottom)]) for zb in range(8)]
    return np.concatenate(turned, axis=0)


def iota(shape, dim):
    return lax.broadcasted_iota(jnp.int32, shape, dim)


def faces_kernel(vel, xlo, xhi, ylo, yhi, zt):
    plane = CY
    comp = CX * CY
    for n, c in enumerate((1, 2)):
        xlo[n * plane : (n + 1) * plane] = vel[c * comp : c * comp + plane]
        xhi[n * plane : (n + 1) * plane] = vel[(c + 1) * comp - plane : (c + 1) * comp]
    for n, c in enumerate((0, 2)):
        ylo[n * CX : (n + 1) * CX] = vel[pl.ds(c * comp, CX, stride=plane)]
        yhi[n * CX : (n + 1) * CX] = vel[pl.ds(c * comp + plane - 1, CX, stride=plane)]
    lane = iota((CY, LANES), 1)
    t = jnp.zeros((CY, LANES), jnp.float32)
    for k in range(2 * CX):
        f = vel[k * plane : (k + 1) * plane]
        t = jnp.where((lane >> 1) == k, pltpu.roll(f, (2 * k + 1) % LANES, 1), t)
    zt[...] = t


def faces(vel2):
    f32 = jnp.float32
    return pl.pallas_call(
        faces_kernel,
        out_shape=[
            jax.ShapeDtypeStruct((2 * CY, LANES), f32),
            jax.ShapeDtypeStruct((2 * CY, LANES), f32),
            jax.ShapeDtypeStruct((2 * CX, LANES), f32),
            jax.ShapeDtypeStruct((2 * CX, LANES), f32),
            jax.ShapeDtypeStruct((CY, LANES), f32),
        ],
        cost_estimate=pl.CostEstimate(flops=4_000_000, bytes_accessed=3_500_000, transcendentals=0),
        compiler_params=pltpu.CompilerParams(vmem_limit_bytes=10 << 20),
        name="faces",
    )(vel2)


def index_kernel(tgt, length, words, wide, head):
    chunks = NBLK // LANES
    t = tgt[...]
    ln = length[...]
    row = iota((WRITERS, LANES), 0)
    before = (iota((LANES, LANES), 0) < iota((LANES, LANES), 1)).astype(jnp.bfloat16)
    ones = jnp.ones((LANES, LANES), jnp.bfloat16)
    rhs = jnp.concatenate([before, ones], axis=1)
    hits, weighted = [], []
    for r in range(chunks):
        hit = t[r : r + 1, :] == row
        hits.append(hit)
        weighted.append(jnp.where(hit, ln[r : r + 1, :], 0).astype(jnp.float32).astype(jnp.bfloat16))
    counted = [jnp.where(h, 1.0, 0.0).astype(jnp.bfloat16) for h in hits]
    nt = (((1,), (1,)), ((), ()))
    base_l = jnp.zeros((WRITERS, LANES), jnp.float32)
    base_c = jnp.zeros((WRITERS, LANES), jnp.float32)
    lens = jnp.zeros((WRITERS, LANES), jnp.float32)
    starts = []
    for r in range(chunks):
        sums_l = jnp.dot(weighted[r], rhs, preferred_element_type=jnp.float32)
        sums_c = jnp.dot(counted[r], rhs, preferred_element_type=jnp.float32)
        start = jnp.where(hits[r], sums_l[:, :LANES] + base_l, 0.0)
        rank = jnp.where(hits[r], sums_c[:, :LANES] + base_c, 0.0)
        starts.append(jnp.sum(start, axis=0, keepdims=True))
        slot = jnp.sum(rank, axis=0, keepdims=True).astype(jnp.int32)
        at = jnp.where(slot == iota((LANES, LANES), 0), 1.0, 0.0).astype(jnp.bfloat16)
        lens += lax.dot_general(weighted[r], at, nt, preferred_element_type=jnp.float32)
        base_l += sums_l[:, LANES:]
        base_c += sums_c[:, LANES:]
    start = jnp.concatenate(starts, axis=0).astype(jnp.int32)
    first = start >> 7
    shift = start & (LANES - 1)
    words[...] = (t * room_of(ROWS) + COMP * jnp.minimum(first, ROWS)) * LANES + shift
    wide[...] = (t * room_of(CAP) + COMP * jnp.minimum(first, CAP)) * LANES + shift
    full = jnp.max(base_l, axis=0, keepdims=True)
    spill = jnp.where(full > ROWS * LANES, 1.0, 0.0)
    lane = iota((WRITERS, LANES), 1)
    head[...] = jnp.where(lane < CAP, lens, jnp.where(lane == CAP + 1, spill, 0.0))


def index(targets, lens):
    i32 = jnp.int32
    return pl.pallas_call(
        index_kernel,
        out_shape=[
            jax.ShapeDtypeStruct((NBLK // LANES, LANES), i32),
            jax.ShapeDtypeStruct((NBLK // LANES, LANES), i32),
            jax.ShapeDtypeStruct((WRITERS, LANES), jnp.float32),
        ],
        cost_estimate=pl.CostEstimate(flops=20_000_000, bytes_accessed=100_000, transcendentals=0),
        compiler_params=pltpu.CompilerParams(vmem_limit_bytes=8 << 20),
        name="index",
    )(targets, lens)


PLANES = 4
PAIR = 2


def curl_kernel(vel, xprev, xnext, yprev, ynext, zprev, znext, head, curls, mine, ends):
    comp = CX * CY
    lane = iota((CY, LANES), 1)
    row = iota((CY, LANES), 0)
    ends[...] = jnp.where(
        (lane & 1) == 0, pltpu.roll(znext[...], LANES - 1, 1), pltpu.roll(zprev[...], 1, 1)
    )
    first, last = lane == 0, lane == LANES - 1

    def plane_of(c, x):
        return vel[pl.ds(pl.multiple_of(c * comp + x * CY, CY), CY)]

    def along_x(c, x, n):
        low = jnp.maximum(x - 1, 0)
        high = jnp.minimum(x + 1, CX - 1)
        below = jnp.where(x == 0, xprev[n * CY : (n + 1) * CY], plane_of(c, low))
        above = jnp.where(x == CX - 1, xnext[n * CY : (n + 1) * CY], plane_of(c, high))
        return above - below

    def along_y(f, x, n):
        above = jnp.where(row == CY - 1, ynext[pl.ds(n * CX + x, CY, stride=0)], pltpu.roll(f, CY - 1, 0))
        below = jnp.where(row == 0, yprev[pl.ds(n * CX + x, CY, stride=0)], pltpu.roll(f, 1, 0))
        return above - below

    def along_z(f, c, x):
        edge = pltpu.roll(ends[...], LANES - 1 - 2 * (c * CX + x), 1)
        above = jnp.where(last, edge, pltpu.roll(f, LANES - 1, 1))
        below = jnp.where(first, edge, pltpu.roll(f, 1, 1))
        return above - below

    def differences(step, total):
        for p in range(PAIR):
            x = step * PAIR + p
            u, v, w = plane_of(0, x), plane_of(1, x), plane_of(2, x)
            curl = (
                along_y(w, x, 1) - along_z(v, 1, x),
                along_z(u, 0, x) - along_x(2, x, 1),
                along_x(1, x, 0) - along_y(u, x, 0),
            )
            for c in range(COMP):
                f = curl[c]
                square = f * f
                for i in range(CY // 8):
                    total += square[i * 8 : (i + 1) * 8]
                curls[pl.ds(pl.multiple_of((x * COMP + c) * CY, CY), CY)] = f
        return total

    total = lax.fori_loop(0, CX // PAIR, differences, jnp.zeros((8, LANES), jnp.float32))
    every = 0.25 * jnp.sum(total, keepdims=True)
    small = iota((8, LANES), 1)
    mine[...] = jnp.where(small == CAP, every, jnp.where(small == CAP + 1, head[0:8, :], 0.0))


def curl_of(vel2, xprev, xnext, yprev, ynext, zprev, znext, head):
    rows = COMP * NBLK
    return pl.pallas_call(
        curl_kernel,
        out_shape=[
            jax.ShapeDtypeStruct((rows, LANES), jnp.float32),
            jax.ShapeDtypeStruct((8, LANES), jnp.float32),
        ],
        scratch_shapes=[pltpu.VMEM((CY, LANES), jnp.float32)],
        cost_estimate=pl.CostEstimate(
            flops=40_000_000, bytes_accessed=7_500_000, transcendentals=0
        ),
        compiler_params=pltpu.CompilerParams(vmem_limit_bytes=16 << 20),
        name="curl",
    )(vel2, xprev, xnext, yprev, ynext, zprev, znext, head)


def transform_kernel(curls, tables, out, tiled):
    granule = iota((8, LANES), 1) >> 4
    count = PLANES * COMP

    def transform(step, carry):
        base = step * (count * CY)
        for n in range(count):
            tiles = []
            for y in range(8):
                f = curls[pl.ds(base + n * CY + (-y) % 8, 8, stride=8)]
                tiles.append(pltpu.roll(f, 16 * ((-y) % 8), 1) if y else f)
            for b in (1, 2, 4):
                moved = (granule & b) != 0
                tiles = [jnp.where(moved, tiles[(j - b) % 8], tiles[j]) for j in range(8)]
            for zb in range(8):
                tiled[zb * count * 8 + n * 8 : zb * count * 8 + n * 8 + 8] = tiles[zb]
        for zb in range(8):
            whole = tiled[zb * count * 8 : (zb + 1) * count * 8]
            high = whole.astype(jnp.bfloat16)
            low = (whole - high.astype(jnp.float32)).astype(jnp.bfloat16)
            both = jnp.dot(
                jnp.concatenate([high, low], axis=1),
                tables[zb * 256 : zb * 256 + 256],
                preferred_element_type=jnp.float32,
            )
            coeffs = both[:, :LANES] + both[:, LANES:]
            for n in range(count):
                p, c = n // COMP, n % COMP
                at = base + COMP * (p * CY + zb * 8) + c
                out[pl.ds(at, 8, stride=COMP)] = coeffs[n * 8 : n * 8 + 8]
        return carry

    lax.fori_loop(0, CX // PLANES, transform, 0)


def transform_of(curls):
    tables = jnp.asarray(tables_np())
    rows = COMP * NBLK
    return pl.pallas_call(
        transform_kernel,
        out_shape=jax.ShapeDtypeStruct((rows, LANES), jnp.float32),
        scratch_shapes=[pltpu.VMEM((PLANES * COMP * CY, LANES), jnp.float32)],
        cost_estimate=pl.CostEstimate(
            flops=2 * rows * 256 * 256, bytes_accessed=7_500_000, transcendentals=0
        ),
        compiler_params=pltpu.CompilerParams(vmem_limit_bytes=16 << 20),
        name="transform",
    )(curls, tables)


def pack_kernel(rows, words, coeffs, head, one, two, three, four, out, room):
    lane = iota((COMP, LANES), 1)
    span, local_span = span_of(rows), room_of(rows)

    def body(r, carry):
        for j in range(LANES):
            p, yb, zb = j // CY, (j % CY) // 8, j % 8
            word = words[r, j]
            addr = word >> 7
            value = coeffs[pl.ds(r * (COMP * LANES) + COMP * (p * CY + zb * 8 + yb), COMP)]
            value = pltpu.roll(value, word, 1)
            kept = lane >= (jnp.full((COMP, LANES), word, jnp.int32) & (LANES - 1))
            pltpu.store(room.at[pl.ds(addr, COMP)], value, mask=kept)
            room[pl.ds(addr + COMP, COMP)] = value
        return carry

    lax.fori_loop(0, NBLK // LANES, body, 0)

    def settle(w, carry):
        source = pl.multiple_of(w * local_span, 8)
        target = pl.multiple_of(w * span, 8)
        out[pl.ds(target, span)] = room[pl.ds(source, span)]
        return carry

    lax.fori_loop(0, WRITERS, settle, 0)
    small = iota((8, LANES), 1)
    both = jnp.where(
        small == CAP,
        (one[...] + two[...]) + (three[...] + four[...]),
        jnp.maximum(jnp.maximum(one[...], two[...]), jnp.maximum(three[...], four[...])),
    )
    for w in range(0, WRITERS, 8):
        out[pl.ds(w * span + COMP * rows, 8, stride=span)] = jnp.where(
            small < CAP, head[w : w + 8], both
        )


def pack(words, coeffs, head, sums, rows):
    span = span_of(rows)
    return pl.pallas_call(
        functools.partial(pack_kernel, rows),
        in_specs=[
            pl.BlockSpec(memory_space=pltpu.SMEM),
            *[pl.BlockSpec(memory_space=pltpu.VMEM)] * 6,
        ],
        out_specs=pl.BlockSpec(memory_space=pltpu.VMEM),
        out_shape=jax.ShapeDtypeStruct((WRITERS * span, LANES), jnp.float32),
        scratch_shapes=[pltpu.VMEM((WRITERS * room_of(rows), LANES), jnp.float32)],
        cost_estimate=pl.CostEstimate(
            flops=200_000_000, bytes_accessed=8_000_000, transcendentals=0
        ),
        compiler_params=pltpu.CompilerParams(vmem_limit_bytes=22 << 20),
        name=f"pack{rows}",
    )(words, coeffs, head, *sums)


SOURCES = 8
ABREAST = 4


def unpack_kernel(rows, head, recv, out, spill, at_s, cut_s, at_v, cut_v, scale, sem):
    step = pl.program_id(0)
    span = span_of(rows)

    @pl.when(step == 0)
    def _():
        h = head[...].reshape(WRITERS, LANES) if head.shape[1] == 1 else head[:, 7, :]
        lane = iota((WRITERS, LANES), 1)
        lens = jnp.where(lane < CAP, h, 0.0)
        before = (iota((LANES, LANES), 0) < iota((LANES, LANES), 1)).astype(jnp.bfloat16)
        start = jnp.dot(lens.astype(jnp.bfloat16), before, preferred_element_type=jnp.float32)
        start = start.astype(jnp.int32)
        first = start >> 7
        turn = start & (LANES - 1)
        at = iota((WRITERS, LANES), 0) * span + COMP * jnp.minimum(first, rows - 2)
        at_v[...] = at * LANES + ((LANES - turn) & (LANES - 1))
        split = jnp.where(first >= rows - 1, LANES, turn)
        cut_v[...] = lens.astype(jnp.int32) + 256 * split
        copies = [
            pltpu.make_async_copy(v, s, sem.at[i])
            for i, (v, s) in enumerate(((at_v, at_s), (cut_v, cut_s)))
        ]
        for copy in copies:
            copy.start()
        total = jnp.sum(jnp.where(lane == CAP, h, 0.0), keepdims=True)
        rms = jnp.sqrt(total * (1.0 / CELLS) + 1e-6)
        scale[...] = jnp.broadcast_to(1.0 / rms, scale.shape)
        flag = jnp.max(jnp.where(lane == CAP + 1, h, 0.0), keepdims=True)
        spill[...] = jnp.broadcast_to(flag, spill.shape).astype(jnp.int32)
        for copy in copies:
            copy.wait()

    factor = scale[0:COMP]
    lane = iota((COMP, LANES), 1)
    flat = out.reshape(COMP * SOURCES * CAP, LANES)

    def body(s, carry):
        for k in range(ABREAST * CAP):
            number, q = step * SOURCES + s * ABREAST + k // CAP, k % CAP
            word = at_s[number, q]
            cut = jnp.full((COMP, LANES), cut_s[number, q], jnp.int32)
            at = word >> 7
            one = recv[pl.ds(at, COMP)]
            two = recv[pl.ds(at + COMP, COMP)]
            value = jnp.where(lane >= (cut >> 8), one, two)
            value = pltpu.roll(value, word, 1)
            value = jnp.where(lane < (cut & 255), value * factor, 0.0)
            flat[pl.ds(s * (ABREAST * CAP) + k, COMP, stride=SOURCES * CAP)] = value
        return carry

    lax.fori_loop(0, SOURCES // ABREAST, body, 0)


def unpack(head, recv, rows):
    if head.shape[1] == 1:
        head_spec = pl.BlockSpec(head.shape, lambda i: (0, 0, 0))
    else:
        head_spec = pl.BlockSpec((WRITERS, 8, LANES), lambda i: (0, head.shape[1] // 8 - 1, 0))
    return pl.pallas_call(
        functools.partial(unpack_kernel, rows),
        grid=(WRITERS // SOURCES,),
        in_specs=[head_spec, pl.BlockSpec(recv.shape, lambda i: (0, 0))],
        out_specs=[
            pl.BlockSpec((COMP, SOURCES * CAP, LANES), lambda i: (0, i, 0)),
            pl.BlockSpec((8, LANES), lambda i: (0, 0)),
        ],
        out_shape=[
            jax.ShapeDtypeStruct((COMP, WRITERS * CAP, LANES), jnp.float32),
            jax.ShapeDtypeStruct((8, LANES), jnp.int32),
        ],
        scratch_shapes=[
            *[pltpu.SMEM((WRITERS, LANES), jnp.int32)] * 2,
            *[pltpu.VMEM((WRITERS, LANES), jnp.int32)] * 2,
            pltpu.VMEM((8, LANES), jnp.float32),
            pltpu.SemaphoreType.DMA((2,)),
        ],
        cost_estimate=pl.CostEstimate(
            flops=200_000_000, bytes_accessed=11_000_000, transcendentals=0
        ),
        compiler_params=pltpu.CompilerParams(vmem_limit_bytes=24 << 20),
        name=f"unpack{rows}",
    )(head, recv)


def exchange(buffer, rows):
    return lax.all_to_all(
        buffer.reshape(WRITERS, span_of(rows), LANES), G, 0, 0, tiled=True
    )


def local(velocity, lengths, destinations):
    vel2 = velocity.reshape(COMP * CX * CY, LANES)
    targets = destinations.reshape(NBLK // LANES, LANES)
    lens = lengths.reshape(NBLK // LANES, LANES)

    xlo, xhi, ylo, yhi, zt = faces(vel2)

    def ring(axis, n, d):
        return functools.partial(
            lax.ppermute, axis_name=axis, perm=[(i, (i + d) % n) for i in range(n)]
        )

    n_x, n_y, n_z = (lax.axis_size(a) for a in ("gx", "gy", "wa"))
    xprev, xnext = ring("gx", n_x, 1)(xhi), ring("gx", n_x, -1)(xlo)
    yprev, ynext = ring("gy", n_y, 1)(yhi), ring("gy", n_y, -1)(ylo)
    zprev, znext = ring("wa", n_z, 1)(zt), ring("wa", n_z, -1)(zt)
    words, wide, head = index(targets, lens)

    curls, mine = curl_of(vel2, xprev, xnext, yprev, ynext, zprev, znext, head)
    sums = [mine] + [ring("wa", n_z, d)(mine) for d in range(1, n_z)]
    coeffs = transform_of(curls)
    packed = pack(words, coeffs, head, sums, ROWS)
    got = exchange(packed, ROWS)
    out, spill = unpack(got, got.reshape(-1, LANES), ROWS)

    def again(carry):
        more = exchange(pack(wide, coeffs, head, sums, CAP), CAP)
        wider, _ = unpack(got[:, COMP * ROWS :, :], more.reshape(-1, LANES), CAP)
        return jnp.int32(0), wider

    _, out = lax.while_loop(lambda carry: carry[0] > 0, again, (spill[0, 0], out))
    return out.reshape(1, 1, COMP, WRITERS, CAP, LANES)


def solution(mesh):
    return jax.shard_map(
        local,
        mesh=mesh,
        in_specs=(
            P(None, "gx", "gy", "wa"),
            P("gx", "gy", "wa", None),
            P("gx", "gy", "wa", None, None),
        ),
        out_specs=P(G, "wa", None, None, None, None),
        check_vma=False,
    )
```

time: 197 us -> 159 us (0.81)
  Pallas kernels: 55.8 us -> 24.8 us
  waiting for transfers between devices: 4.4 us -> 0.04 us
  starting transfers between devices: 11.3 us -> 15.1 us
  other arithmetic: 2.66 us -> 0 us
    pallas_call x4, Pallas kernels: 50.5 us -> 23.4 us  [the longest x1 11.9 us: unpack(): pl.pallas_call(functools.partial(unpack_kernel, rows), grid=(WRITERS // S...]
    ppermute x2 -> x3, starting transfers between devices: 0.42 us -> 3.85 us  [local(): sums = [mine] + [ring('wa', n_z, d)(mine) for d in range(1, n_z)]]
    pallas_call x1, Pallas kernels: 3.11 us -> 0.61 us  [faces(): pl.pallas_call(faces_kernel, out_shape=[jax.ShapeDtypeStruct((2 * CY, LAN...]
    ppermute x2 -> x3, waiting for transfers between devices: 2.41 us -> 0.01 us  [local(): sums = [mine] + [ring('wa', n_z, d)(mine) for d in range(1, n_z)]]
    unnamed x16 -> x12, local copies, waits for them, and re-layouts: 3.26 us -> 5.17 us
  transfers between devices with their start and end apart: 8 -> 9, of which waited for: 2 -> 0; matrix products, arithmetic and copies ran while one was open for 0% -> 0% of each run, Pallas kernels for 8% -> 2%
where the time goes in v2:
time: 159 us
  blocking collectives  113 us (71%)
  Pallas kernels  24.8 us (16%)
  starting transfers between devices  15.1 us (9%)
  local copies, waits for them, and re-layouts  5.71 us (4%)
    all_to_all x1, blocking collectives, exchange(): lax.all_to_all(buffer.reshape(WRITERS, span_of(rows), LANES), G, 0, 0, ti...  113 us
    pallas_call x1, Pallas kernels, unpack(): pl.pallas_call(functools.partial(unpack_kernel, rows), grid=(WRITERS // S...  11.9 us
    pallas_call x1, Pallas kernels, pack(): pl.pallas_call(functools.partial(pack_kernel, rows), in_specs=[pl.BlockSp...  5.25 us
    unnamed x12, local copies, waits for them, and re-layouts  5.17 us
    ppermute x2, starting transfers between devices, local(): yprev, ynext = (ring('gy', n_y, 1)(yhi), ring('gy', n_y, -1)(ylo))  4.97 us
    ppermute x2, starting transfers between devices, local(): zprev, znext = (ring('wa', n_z, 1)(zt), ring('wa', n_z, -1)(zt))  4.18 us
    ppermute x3, starting transfers between devices, local(): sums = [mine] + [ring('wa', n_z, d)(mine) for d in range(1, n_z)]  3.85 us
  transfers between devices with their start and end apart: 9, of which 0 were waited for; matrix products, arithmetic and copies ran while one was open for 0% of the time, Pallas kernels for 2%

profile of v2, /device:TPU:1, one launch (start us, length us, event | category | flops | bytes accessed | tf_op | source)
XLA Modules:
  0.0 159.2 jit_solution(5203649021410127473)
XLA Ops:
  0.0 0.0 copy-start.1
  0.0 1.9 %copy-done.1 = f32[3,32,64,128]{3,2,1,0:T(8,128)S(1)} copy-done((f32[3,32,64,128]{3,2,1,0:T(8,128)S(1)}, f32[3,32,64,128]{3,2,1,0:T(8,128)}, u32[]{:S(2)}) %copy-start.1) | copy-done | bytes 3145752
  1.9 0.0 copy-start.3
  1.9 0.6 faces.1
  2.5 2.2 %collective-permute-start.4 = (f32[64,128]{1,0:T(8,128)S(1)}, f32[64,128]{1,0:T(8,128)S(1)}, u32[]{:S(2)}, u32[]{:S(2)}) collective-permute-start(f32[64,128]{1,0:T(8,128)S(1)} %get-tuple-element.73), channel_id=1, source_target_pairs={{0,1},{1,2},{2,3},{3,0},{4,5},{5,6},{6,7},{7,4},{8,9},{9,10},{10,1... | collective-permute-start | bytes 98312 | tf_op jit(solution)/shard_map/ppermute | solution.py:434
  4.7 2.1 %collective-permute-start = (f32[128,128]{1,0:T(8,128)S(1)}, f32[128,128]{1,0:T(8,128)S(1)}, u32[]{:S(2)}, u32[]{:S(2)}) collective-permute-start(f32[128,128]{1,0:T(8,128)S(1)} %get-tuple-element.69), channel_id=1, source_target_pairs={{0,32},{32,64},{64,96},{96,128},{128,160},{160,192},{192,224},{224... | collective-permute-start | bytes 196616 | tf_op jit(solution)/shard_map/ppermute | solution.py:432
  6.8 0.0 collective-permute-start.1
  6.8 2.0 %collective-permute-start.5 = (f32[64,128]{1,0:T(8,128)S(1)}, f32[64,128]{1,0:T(8,128)S(1)}, u32[]{:S(2)}, u32[]{:S(2)}) collective-permute-start(f32[64,128]{1,0:T(8,128)S(1)} %get-tuple-element.73), channel_id=1, source_target_pairs={{0,3},{1,0},{2,1},{3,2},{4,7},{5,4},{6,5},{7,6},{8,11},{9,8},{10,9... | collective-permute-start | bytes 98312 | tf_op jit(solution)/shard_map/ppermute | solution.py:434
  8.8 1.0 collective-permute-start.2
  9.8 0.0 collective-permute-done.4.zprev
  9.8 3.9 %collective-permute-start.3 = (f32[64,128]{1,0:T(8,128)S(1)}, f32[64,128]{1,0:T(8,128)S(1)}, u32[]{:S(2)}, u32[]{:S(2)}) collective-permute-start(f32[64,128]{1,0:T(8,128)S(1)} %get-tuple-element.72), channel_id=1, source_target_pairs={{0,28},{4,0},{8,4},{12,8},{16,12},{20,16},{24,20},{28,24},{1,29},{... | collective-permute-start | bytes 98312 | tf_op jit(solution)/shard_map/ppermute | solution.py:433
  13.7 0.0 copy-start.4
  13.7 0.7 copy-done.4
  14.4 0.0 copy-start.5
  14.4 0.7 copy-done.5
  15.1 0.8 index.1
  15.9 0.0 collective-permute-done.5.znext
  16.0 0.0 collective-permute-done.2.yprev
  16.0 0.0 collective-permute-done.3.ynext
  16.0 0.0 collective-permute-done.xprev
  16.0 0.0 collective-permute-done.1.xnext
  16.0 0.0 copy-start.2
  16.0 1.9 %copy-done.2 = f32[3,32,64,128]{3,2,1,0:T(8,128)S(1)} copy-done((f32[3,32,64,128]{3,2,1,0:T(8,128)S(1)}, f32[3,32,64,128]{3,2,1,0:T(8,128)}, u32[]{:S(2)}) %copy-start.2) | copy-done | bytes 3145752
  17.9 3.1 %curl.1 = (f32[6144,128]{1,0:T(8,128)S(1)}, f32[8,128]{1,0:T(8,128)S(1)}) custom-call(f32[6144,128]{1,0:T(8,128)S(1)} %bitcast.12, f32[128,128]{1,0:T(8,128)S(1)} %collective-permute-done.xprev, f32[128,128]{1,0:T(8,128)S(1)} %collective-permute-done.1.xnext, f32[64,128]{1,0:T(8,128)S(1)} %collective-permute-done.2.yprev, ...), custom_call_target="tpu_custom_call" | custom-call | flops 40000000 | bytes 7500000 | tf_op jit(solution)/shard_map/curl/pallas_call | solution.py:204
  21.0 0.2 collective-permute-start.6
  21.2 2.6 %collective-permute-start.7 = (f32[8,128]{1,0:T(8,128)S(1)}, f32[8,128]{1,0:T(8,128)S(1)}, u32[]{:S(2)}, u32[]{:S(2)}) collective-permute-start(f32[8,128]{1,0:T(8,128)S(1)} %get-tuple-element.117.one), channel_id=1, source_target_pairs={{0,2},{1,3},{2,0},{3,1},{4,6},{5,7},{6,4},{7,5},{8,10},{9,11},{10,... | collective-permute-start | bytes 12296 | tf_op jit(solution)/shard_map/ppermute | solution.py:438
  23.8 1.1 collective-permute-start.8
  24.9 0.0 copy-done.3
  24.9 3.2 %transform.1.coeffs = f32[6144,128]{1,0:T(8,128)S(1)} custom-call(f32[6144,128]{1,0:T(8,128)S(1)} %get-tuple-element.75.curls, bf16[2048,256]{1,0:T(8,128)(2,1)S(1)} %copy-done.3), custom_call_target="tpu_custom_call" | custom-call | flops 805306368 | bytes 7500000 | tf_op jit(solution)/shard_map/transform/pallas_call | solution.py:257
  28.1 0.0 collective-permute-done.6.two
  28.1 0.0 collective-permute-done.7.three
  28.1 0.0 collective-permute-done.8.four
  28.1 5.3 %pack45.1 = f32[8704,128]{1,0:T(8,128)S(1)} custom-call(s32[16,128]{1,0:T(8,128)S(1)} %get-tuple-element.68.words, f32[6144,128]{1,0:T(8,128)S(1)} %transform.1.coeffs, f32[64,128]{1,0:T(8,128)S(1)} %get-tuple-element.116.head, f32[8,128]{1,0:T(8,128)S(1)} %get-tuple-element.117.one, f32[8,128]{1,0:T(8,128)S(1)} %collective-permute-done.6.two, ...), custom_call_target="tpu_custom_call" | custom-call | flops 200000000 | bytes 8000000 | tf_op jit(solution)/shard_map/pack45/pallas_call | solution.py:308
  33.4 112.8 %all_to_all.9.head = f32[64,136,128]{2,1,0:T(8,128)S(1)} all-to-all(f32[64,136,128]{2,1,0:T(8,128)S(1)} %bitcast.10), channel_id=1, replica_groups=mesh['gx'=8,'gy'=8,'wa'=4] {'gx','gy'}, dimensions={0} | all-to-all | bytes 8912896 | tf_op jit(solution)/shard_map/all_to_all | solution.py:414
  146.1 0.0 copy-start.6
  146.1 11.9 %unpack45.1 = (f32[3,4096,128]{2,1,0:T(8,128)}, s32[8,128]{1,0:T(8,128)S(1)}) custom-call(f32[64,136,128]{2,1,0:T(8,128)S(1)} %all_to_all.9.head, f32[8704,128]{1,0:T(8,128)S(1)} %bitcast.15), custom_call_target="tpu_custom_call" | custom-call | flops 200000000 | bytes 11000000 | tf_op jit(solution)/shard_map/unpack45/pallas_call | solution.py:387
  158.0 0.5 slice.6
  158.5 0.0 copy-done.6
  158.5 0.6 while.9
Async XLA Ops:
  0.0 1.9 %copy-start.1 = (f32[3,32,64,128]{3,2,1,0:T(8,128)S(1)}, f32[3,32,64,128]{3,2,1,0:T(8,128)}, u32[]{:S(2)}) copy-start(f32[3,32,64,128]{3,2,1,0:T(8,128)} %param.6) | copy-start | bytes 9437188
  1.9 23.0 %copy-start.3 = (bf16[2048,256]{1,0:T(8,128)(2,1)S(1)}, bf16[2048,256]{1,0:T(8,128)(2,1)}, u32[]{:S(2)}) copy-start(bf16[2048,256]{1,0:T(8,128)(2,1)} %constant.6.clone.tables) | copy-start | bytes 3145732
  2.5 7.3 %collective-permute-start.4 = (f32[64,128]{1,0:T(8,128)S(1)}, f32[64,128]{1,0:T(8,128)S(1)}, u32[]{:S(2)}, u32[]{:S(2)}) collective-permute-start(f32[64,128]{1,0:T(8,128)S(1)} %get-tuple-element.73), channel_id=1, source_target_pairs={{0,1},{1,2},{2,3},{3,0},{4,5},{5,6},{6,7},{7,4},{8,9},{9,10},{10,1... | collective-permute-start | bytes 98312 | tf_op jit(solution)/shard_map/ppermute | solution.py:434
  4.7 11.3 %collective-permute-start = (f32[128,128]{1,0:T(8,128)S(1)}, f32[128,128]{1,0:T(8,128)S(1)}, u32[]{:S(2)}, u32[]{:S(2)}) collective-permute-start(f32[128,128]{1,0:T(8,128)S(1)} %get-tuple-element.69), channel_id=1, source_target_pairs={{0,32},{32,64},{64,96},{96,128},{128,160},{160,192},{192,224},{224... | collective-permute-start | bytes 196616 | tf_op jit(solution)/shard_map/ppermute | solution.py:432
  6.8 9.2 %collective-permute-start.1 = (f32[128,128]{1,0:T(8,128)S(1)}, f32[128,128]{1,0:T(8,128)S(1)}, u32[]{:S(2)}, u32[]{:S(2)}) collective-permute-start(f32[128,128]{1,0:T(8,128)S(1)} %get-tuple-element.70), channel_id=1, source_target_pairs={{0,224},{32,0},{64,32},{96,64},{128,96},{160,128},{192,160},{224,1... | collective-permute-start | bytes 196616 | tf_op jit(solution)/shard_map/ppermute | solution.py:432
  6.8 9.2 %collective-permute-start.5 = (f32[64,128]{1,0:T(8,128)S(1)}, f32[64,128]{1,0:T(8,128)S(1)}, u32[]{:S(2)}, u32[]{:S(2)}) collective-permute-start(f32[64,128]{1,0:T(8,128)S(1)} %get-tuple-element.73), channel_id=1, source_target_pairs={{0,3},{1,0},{2,1},{3,2},{4,7},{5,4},{6,5},{7,6},{8,11},{9,8},{10,9... | collective-permute-start | bytes 98312 | tf_op jit(solution)/shard_map/ppermute | solution.py:434
  8.8 7.2 %collective-permute-start.2 = (f32[64,128]{1,0:T(8,128)S(1)}, f32[64,128]{1,0:T(8,128)S(1)}, u32[]{:S(2)}, u32[]{:S(2)}) collective-permute-start(f32[64,128]{1,0:T(8,128)S(1)} %get-tuple-element.71), channel_id=1, source_target_pairs={{0,4},{4,8},{8,12},{12,16},{16,20},{20,24},{24,28},{28,0},{1,5},{5... | collective-permute-start | bytes 98312 | tf_op jit(solution)/shard_map/ppermute | solution.py:433
  9.8 6.2 %collective-permute-start.3 = (f32[64,128]{1,0:T(8,128)S(1)}, f32[64,128]{1,0:T(8,128)S(1)}, u32[]{:S(2)}, u32[]{:S(2)}) collective-permute-start(f32[64,128]{1,0:T(8,128)S(1)} %get-tuple-element.72), channel_id=1, source_target_pairs={{0,28},{4,0},{8,4},{12,8},{16,12},{20,16},{24,20},{28,24},{1,29},{... | collective-permute-start | bytes 98312 | tf_op jit(solution)/shard_map/ppermute | solution.py:433
  13.7 0.7 copy-start.4
  14.4 0.7 copy-start.5
  16.0 1.9 %copy-start.2 = (f32[3,32,64,128]{3,2,1,0:T(8,128)S(1)}, f32[3,32,64,128]{3,2,1,0:T(8,128)}, u32[]{:S(2)}) copy-start(f32[3,32,64,128]{3,2,1,0:T(8,128)} %param.6) | copy-start | bytes 9437188
  21.0 7.0 %collective-permute-start.6 = (f32[8,128]{1,0:T(8,128)S(1)}, f32[8,128]{1,0:T(8,128)S(1)}, u32[]{:S(2)}, u32[]{:S(2)}) collective-permute-start(f32[8,128]{1,0:T(8,128)S(1)} %get-tuple-element.117.one), channel_id=1, source_target_pairs={{0,1},{1,2},{2,3},{3,0},{4,5},{5,6},{6,7},{7,4},{8,9},{9,10},{10,1... | collective-permute-start | bytes 12296 | tf_op jit(solution)/shard_map/ppermute | solution.py:438
  21.2 6.9 %collective-permute-start.7 = (f32[8,128]{1,0:T(8,128)S(1)}, f32[8,128]{1,0:T(8,128)S(1)}, u32[]{:S(2)}, u32[]{:S(2)}) collective-permute-start(f32[8,128]{1,0:T(8,128)S(1)} %get-tuple-element.117.one), channel_id=1, source_target_pairs={{0,2},{1,3},{2,0},{3,1},{4,6},{5,7},{6,4},{7,5},{8,10},{9,11},{10,... | collective-permute-start | bytes 12296 | tf_op jit(solution)/shard_map/ppermute | solution.py:438
  23.8 4.3 %collective-permute-start.8 = (f32[8,128]{1,0:T(8,128)S(1)}, f32[8,128]{1,0:T(8,128)S(1)}, u32[]{:S(2)}, u32[]{:S(2)}) collective-permute-start(f32[8,128]{1,0:T(8,128)S(1)} %get-tuple-element.117.one), channel_id=1, source_target_pairs={{0,3},{1,0},{2,1},{3,2},{4,7},{5,4},{6,5},{7,6},{8,11},{9,8},{10,9... | collective-permute-start | bytes 12296 | tf_op jit(solution)/shard_map/ppermute | solution.py:438
  146.1 12.4 %copy-start.6 = (f32[64,136,128]{2,1,0:T(8,128)}, f32[64,136,128]{2,1,0:T(8,128)S(1)}, u32[]{:S(2)}) copy-start(f32[64,136,128]{2,1,0:T(8,128)S(1)} %all_to_all.9.head) | copy-start | bytes 13369348

commit v3 on v2

--- a/solution.py
+++ b/solution.py
@@ -52,7 +52,7 @@
     return lax.broadcasted_iota(jnp.int32, shape, dim)
 
 
-def faces_kernel(vel, xlo, xhi, ylo, yhi, zt):
+def faces_kernel(vel, xlo, xhi, ylo, yhi, zt, held):
     plane = CY
     comp = CX * CY
     for n, c in enumerate((1, 2)):
@@ -67,6 +67,7 @@
         f = vel[k * plane : (k + 1) * plane]
         t = jnp.where((lane >> 1) == k, pltpu.roll(f, (2 * k + 1) % LANES, 1), t)
     zt[...] = t
+    held[...] = vel[...]
 
 
 def faces(vel2):
@@ -79,6 +80,7 @@
             jax.ShapeDtypeStruct((2 * CX, LANES), f32),
             jax.ShapeDtypeStruct((2 * CX, LANES), f32),
             jax.ShapeDtypeStruct((CY, LANES), f32),
+            jax.ShapeDtypeStruct(vel2.shape, f32),
         ],
         cost_estimate=pl.CostEstimate(flops=4_000_000, bytes_accessed=3_500_000, transcendentals=0),
         compiler_params=pltpu.CompilerParams(vmem_limit_bytes=10 << 20),
@@ -86,10 +88,10 @@
     )(vel2)
 
 
-def index_kernel(tgt, length, words, wide, head):
+def index_kernel(mixed, words, wide, head):
     chunks = NBLK // LANES
-    t = tgt[...]
-    ln = length[...]
+    t = mixed[...] >> 8
+    ln = mixed[...] & 255
     row = iota((WRITERS, LANES), 0)
     before = (iota((LANES, LANES), 0) < iota((LANES, LANES), 1)).astype(jnp.bfloat16)
     ones = jnp.ones((LANES, LANES), jnp.bfloat16)
@@ -127,7 +129,7 @@
     head[...] = jnp.where(lane < CAP, lens, jnp.where(lane == CAP + 1, spill, 0.0))
 
 
-def index(targets, lens):
+def index(mixed):
     i32 = jnp.int32
     return pl.pallas_call(
         index_kernel,
@@ -139,7 +141,7 @@
         cost_estimate=pl.CostEstimate(flops=20_000_000, bytes_accessed=100_000, transcendentals=0),
         compiler_params=pltpu.CompilerParams(vmem_limit_bytes=8 << 20),
         name="index",
-    )(targets, lens)
+    )(mixed)
 
 
 PLANES = 4
@@ -266,23 +268,27 @@
     )(curls, tables)
 
 
+WIDTH = 2
+
+
 def pack_kernel(rows, words, coeffs, head, one, two, three, four, out, room):
     lane = iota((COMP, LANES), 1)
     span, local_span = span_of(rows), room_of(rows)
 
     def body(r, carry):
-        for j in range(LANES):
+        for j in range(WIDTH * LANES):
             p, yb, zb = j // CY, (j % CY) // 8, j % 8
-            word = words[r, j]
+            word = words[r * WIDTH + j // LANES, j % LANES]
             addr = word >> 7
-            value = coeffs[pl.ds(r * (COMP * LANES) + COMP * (p * CY + zb * 8 + yb), COMP)]
+            source = COMP * (p * CY + zb * 8 + yb)
+            value = coeffs[pl.ds(r * (COMP * WIDTH * LANES) + source, COMP)]
             value = pltpu.roll(value, word, 1)
             kept = lane >= (jnp.full((COMP, LANES), word, jnp.int32) & (LANES - 1))
             pltpu.store(room.at[pl.ds(addr, COMP)], value, mask=kept)
             room[pl.ds(addr + COMP, COMP)] = value
         return carry
 
-    lax.fori_loop(0, NBLK // LANES, body, 0)
+    lax.fori_loop(0, NBLK // LANES // WIDTH, body, 0)
 
     def settle(w, carry):
         source = pl.multiple_of(w * local_span, 8)
@@ -323,16 +329,24 @@
 
 
 SOURCES = 8
-ABREAST = 4
-
-
-def unpack_kernel(rows, head, recv, out, spill, at_s, cut_s, at_v, cut_v, scale, sem):
+ABREAST = 8
+
+
+def unpack_kernel(rows, *refs):
+    head = None
+    if len(refs) == 10:
+        head, refs = refs[0], refs[1:]
+    recv, out, spill, heads, words_s, words_v, scale, pieces, sem = refs
     step = pl.program_id(0)
     span = span_of(rows)
 
     @pl.when(step == 0)
     def _():
-        h = head[...].reshape(WRITERS, LANES) if head.shape[1] == 1 else head[:, 7, :]
+        if head is None:
+            h = recv[pl.ds(COMP * rows, WRITERS, stride=span)]
+        else:
+            h = head[...]
+        heads[...] = h
         lane = iota((WRITERS, LANES), 1)
         lens = jnp.where(lane < CAP, h, 0.0)
         before = (iota((LANES, LANES), 0) < iota((LANES, LANES), 1)).astype(jnp.bfloat16)
@@ -341,73 +355,72 @@
         first = start >> 7
         turn = start & (LANES - 1)
         at = iota((WRITERS, LANES), 0) * span + COMP * jnp.minimum(first, rows - 2)
-        at_v[...] = at * LANES + ((LANES - turn) & (LANES - 1))
-        split = jnp.where(first >= rows - 1, LANES, turn)
-        cut_v[...] = lens.astype(jnp.int32) + 256 * split
-        copies = [
-            pltpu.make_async_copy(v, s, sem.at[i])
-            for i, (v, s) in enumerate(((at_v, at_s), (cut_v, cut_s)))
-        ]
-        for copy in copies:
-            copy.start()
+        late = (first >= rows - 1).astype(jnp.int32)
+        words_v[...] = (
+            (at << 17) + (lens.astype(jnp.int32) << 9) + (late << 8) + (LANES - turn)
+        )
+        copy = pltpu.make_async_copy(words_v, words_s, sem)
+        copy.start()
         total = jnp.sum(jnp.where(lane == CAP, h, 0.0), keepdims=True)
         rms = jnp.sqrt(total * (1.0 / CELLS) + 1e-6)
         scale[...] = jnp.broadcast_to(1.0 / rms, scale.shape)
-        flag = jnp.max(jnp.where(lane == CAP + 1, h, 0.0), keepdims=True)
-        spill[...] = jnp.broadcast_to(flag, spill.shape).astype(jnp.int32)
-        for copy in copies:
-            copy.wait()
-
-    factor = scale[0:COMP]
+        spill[0, 0] = jnp.max(jnp.where(lane == CAP + 1, h, 0.0)).astype(jnp.int32)
+        copy.wait()
+
+    factor = scale[...]
     lane = iota((COMP, LANES), 1)
-    flat = out.reshape(COMP * SOURCES * CAP, LANES)
 
     def body(s, carry):
         for k in range(ABREAST * CAP):
             number, q = step * SOURCES + s * ABREAST + k // CAP, k % CAP
-            word = at_s[number, q]
-            cut = jnp.full((COMP, LANES), cut_s[number, q], jnp.int32)
-            at = word >> 7
+            word = words_s[number, q]
+            marks = jnp.full((COMP, LANES), word, jnp.int32)
+            at = word >> 17
             one = recv[pl.ds(at, COMP)]
             two = recv[pl.ds(at + COMP, COMP)]
-            value = jnp.where(lane >= (cut >> 8), one, two)
+            inside = ((marks & 511) + lane) & 384
+            value = jnp.where(inside == LANES, one, two)
             value = pltpu.roll(value, word, 1)
-            value = jnp.where(lane < (cut & 255), value * factor, 0.0)
-            flat[pl.ds(s * (ABREAST * CAP) + k, COMP, stride=SOURCES * CAP)] = value
+            value = jnp.where(lane < ((marks >> 9) & 255), value, 0.0)
+            pieces[k * 4 : k * 4 + COMP] = value
+        for k in range(0, ABREAST * CAP, 8):
+            for c in range(COMP):
+                row = pl.multiple_of(s * (ABREAST * CAP) + k, 8)
+                out[c, pl.ds(row, 8)] = pieces[pl.ds(k * 4 + c, 8, stride=4)] * factor
         return carry
 
     lax.fori_loop(0, SOURCES // ABREAST, body, 0)
 
 
-def unpack(head, recv, rows):
-    if head.shape[1] == 1:
-        head_spec = pl.BlockSpec(head.shape, lambda i: (0, 0, 0))
-    else:
-        head_spec = pl.BlockSpec((WRITERS, 8, LANES), lambda i: (0, head.shape[1] // 8 - 1, 0))
+def unpack(recv, rows, head=None):
+    args = (recv,) if head is None else (head, recv)
     return pl.pallas_call(
         functools.partial(unpack_kernel, rows),
         grid=(WRITERS // SOURCES,),
-        in_specs=[head_spec, pl.BlockSpec(recv.shape, lambda i: (0, 0))],
+        in_specs=[pl.BlockSpec(a.shape, lambda i: (0, 0)) for a in args],
         out_specs=[
             pl.BlockSpec((COMP, SOURCES * CAP, LANES), lambda i: (0, i, 0)),
-            pl.BlockSpec((8, LANES), lambda i: (0, 0)),
+            pl.BlockSpec(memory_space=pltpu.SMEM),
+            pl.BlockSpec((WRITERS, LANES), lambda i: (0, 0)),
         ],
         out_shape=[
             jax.ShapeDtypeStruct((COMP, WRITERS * CAP, LANES), jnp.float32),
-            jax.ShapeDtypeStruct((8, LANES), jnp.int32),
+            jax.ShapeDtypeStruct((1, 1), jnp.int32),
+            jax.ShapeDtypeStruct((WRITERS, LANES), jnp.float32),
         ],
         scratch_shapes=[
-            *[pltpu.SMEM((WRITERS, LANES), jnp.int32)] * 2,
-            *[pltpu.VMEM((WRITERS, LANES), jnp.int32)] * 2,
+            pltpu.SMEM((WRITERS, LANES), jnp.int32),
+            pltpu.VMEM((WRITERS, LANES), jnp.int32),
             pltpu.VMEM((8, LANES), jnp.float32),
-            pltpu.SemaphoreType.DMA((2,)),
+            pltpu.VMEM((ABREAST * CAP * 4, LANES), jnp.float32),
+            pltpu.SemaphoreType.DMA,
         ],
         cost_estimate=pl.CostEstimate(
             flops=200_000_000, bytes_accessed=11_000_000, transcendentals=0
         ),
         compiler_params=pltpu.CompilerParams(vmem_limit_bytes=24 << 20),
         name=f"unpack{rows}",
-    )(head, recv)
+    )(*args)
 
 
 def exchange(buffer, rows):
@@ -421,7 +434,7 @@
     targets = destinations.reshape(NBLK // LANES, LANES)
     lens = lengths.reshape(NBLK // LANES, LANES)
 
-    xlo, xhi, ylo, yhi, zt = faces(vel2)
+    xlo, xhi, ylo, yhi, zt, vel2 = faces(vel2)
 
     def ring(axis, n, d):
         return functools.partial(
@@ -432,21 +445,21 @@
     xprev, xnext = ring("gx", n_x, 1)(xhi), ring("gx", n_x, -1)(xlo)
     yprev, ynext = ring("gy", n_y, 1)(yhi), ring("gy", n_y, -1)(ylo)
     zprev, znext = ring("wa", n_z, 1)(zt), ring("wa", n_z, -1)(zt)
-    words, wide, head = index(targets, lens)
+    words, wide, head = index(targets * 256 + lens)
 
     curls, mine = curl_of(vel2, xprev, xnext, yprev, ynext, zprev, znext, head)
     sums = [mine] + [ring("wa", n_z, d)(mine) for d in range(1, n_z)]
     coeffs = transform_of(curls)
     packed = pack(words, coeffs, head, sums, ROWS)
     got = exchange(packed, ROWS)
-    out, spill = unpack(got, got.reshape(-1, LANES), ROWS)
+    out, spill, heads = unpack(got.reshape(-1, LANES), ROWS)
 
     def again(carry):
         more = exchange(pack(wide, coeffs, head, sums, CAP), CAP)
-        wider, _ = unpack(got[:, COMP * ROWS :, :], more.reshape(-1, LANES), CAP)
+        wider, _, _ = unpack(more.reshape(-1, LANES), CAP, heads)
         return jnp.int32(0), wider
 
-    _, out = lax.while_loop(lambda carry: carry[0] > 0, again, (spill[0, 0], out))
+    _, out = lax.while_loop(lambda carry: carry[0] > 0, again, (spill.reshape(()), out))
     return out.reshape(1, 1, COMP, WRITERS, CAP, LANES)
 
 

time: 159 us -> 156 us (0.981)
  local copies, waits for them, and re-layouts: 5.71 us -> 1.89 us
    unnamed x12 -> x4, local copies, waits for them, and re-layouts: 5.17 us -> 1.89 us
  transfers between devices with their start and end apart: 9 -> 9, of which waited for: 0 -> 0; matrix products, arithmetic and copies ran while one was open for 0% -> 1% of each run, Pallas kernels for 2% -> 3%
where the time goes in v3:
time: 156 us; the launch traced here: 155 us
  blocking collectives  112 us (72%)
  Pallas kernels  23.3 us (15%)
  starting transfers between devices  15.4 us (10%)
  local copies, waits for them, and re-layouts  1.89 us (1%)
    all_to_all x1, blocking collectives, exchange(): lax.all_to_all(buffer.reshape(WRITERS, span_of(rows), LANES), G, 0, 0, ti...  112 us
    pallas_call x1, Pallas kernels, unpack(): pl.pallas_call(functools.partial(unpack_kernel, rows), grid=(WRITERS // S...  10.4 us
    ppermute x2, starting transfers between devices, local(): yprev, ynext = (ring('gy', n_y, 1)(yhi), ring('gy', n_y, -1)(ylo))  5.05 us
    pallas_call x1, Pallas kernels, pack(): pl.pallas_call(functools.partial(pack_kernel, rows), in_specs=[pl.BlockSp...  5.02 us
    ppermute x3, starting transfers between devices, local(): sums = [mine] + [ring('wa', n_z, d)(mine) for d in range(1, n_z)]  3.85 us
    ppermute x2, starting transfers between devices, local(): zprev, znext = (ring('wa', n_z, 1)(zt), ring('wa', n_z, -1)(zt))  3.72 us
    pallas_call x1, Pallas kernels, transform_of(): pl.pallas_call(transform_kernel, out_shape=jax.ShapeDtypeStruct((rows, LA...  3.16 us
    pallas_call x1, Pallas kernels, curl_of(): pl.pallas_call(curl_kernel, out_shape=[jax.ShapeDtypeStruct((rows, LANES)...  3.13 us
  transfers between devices with their start and end apart: 9, of which 0 were waited for; matrix products, arithmetic and copies ran while one was open for 1% of the time, Pallas kernels for 3%

profile of v3, /device:TPU:1, one launch (start us, length us, event | category | flops | bytes accessed | tf_op | source)
XLA Modules:
  0.0 155.5 jit_solution(15518689021455236199)
XLA Ops:
  0.0 0.0 copy-start.1
  0.0 1.9 %copy-done.1 = f32[3,32,64,128]{3,2,1,0:T(8,128)S(1)} copy-done((f32[3,32,64,128]{3,2,1,0:T(8,128)S(1)}, f32[3,32,64,128]{3,2,1,0:T(8,128)}, u32[]{:S(2)}) %copy-start.1) | copy-done | bytes 3145752
  1.9 0.0 copy-start.2
  1.9 0.8 faces.1
  2.7 2.2 %collective-permute-start.4 = (f32[64,128]{1,0:T(8,128)S(1)}, f32[64,128]{1,0:T(8,128)S(1)}, u32[]{:S(2)}, u32[]{:S(2)}) collective-permute-start(f32[64,128]{1,0:T(8,128)S(1)} %get-tuple-element.76), channel_id=1, source_target_pairs={{0,1},{1,2},{2,3},{3,0},{4,5},{5,6},{6,7},{7,4},{8,9},{9,10},{10,1... | collective-permute-start | bytes 98312 | tf_op jit(solution)/shard_map/ppermute | solution.py:447
  4.9 1.5 collective-permute-start.5
  6.4 2.2 %collective-permute-start = (f32[128,128]{1,0:T(8,128)S(1)}, f32[128,128]{1,0:T(8,128)S(1)}, u32[]{:S(2)}, u32[]{:S(2)}) collective-permute-start(f32[128,128]{1,0:T(8,128)S(1)} %get-tuple-element.72), channel_id=1, source_target_pairs={{0,32},{32,64},{64,96},{96,128},{128,160},{160,192},{192,224},{224... | collective-permute-start | bytes 196616 | tf_op jit(solution)/shard_map/ppermute | solution.py:445
  8.6 0.6 collective-permute-start.1
  9.2 1.0 collective-permute-start.2
  10.2 0.0 collective-permute-done.4.zprev
  10.2 4.0 %collective-permute-start.3 = (f32[64,128]{1,0:T(8,128)S(1)}, f32[64,128]{1,0:T(8,128)S(1)}, u32[]{:S(2)}, u32[]{:S(2)}) collective-permute-start(f32[64,128]{1,0:T(8,128)S(1)} %get-tuple-element.75), channel_id=1, source_target_pairs={{0,28},{4,0},{8,4},{12,8},{16,12},{20,16},{24,20},{28,24},{1,29},{... | collective-permute-start | bytes 98312 | tf_op jit(solution)/shard_map/ppermute | solution.py:446
  14.2 0.7 broadcast_multiply_fusion
  15.0 0.7 add.3.mixed
  15.7 0.8 index.1
  16.5 0.0 collective-permute-done.5.znext
  16.5 0.0 collective-permute-done.2.yprev
  16.5 0.0 collective-permute-done.3.ynext
  16.5 0.0 collective-permute-done.xprev
  16.5 0.0 collective-permute-done.1.xnext
  16.5 3.1 %curl.1 = (f32[6144,128]{1,0:T(8,128)S(1)}, f32[8,128]{1,0:T(8,128)S(1)}) custom-call(f32[6144,128]{1,0:T(8,128)S(1)} %get-tuple-element.71.vel, f32[128,128]{1,0:T(8,128)S(1)} %collective-permute-done.xprev, f32[128,128]{1,0:T(8,128)S(1)} %collective-permute-done.1.xnext, f32[64,128]{1,0:T(8,128)S(1)} %collective-permute-done.2.yprev, ...), custom_call_target="tpu_custom_call" | custom-call | flops 40000000 | bytes 7500000 | tf_op jit(solution)/shard_map/curl/pallas_call | solution.py:206
  19.7 0.2 collective-permute-start.6
  19.8 2.6 %collective-permute-start.7 = (f32[8,128]{1,0:T(8,128)S(1)}, f32[8,128]{1,0:T(8,128)S(1)}, u32[]{:S(2)}, u32[]{:S(2)}) collective-permute-start(f32[8,128]{1,0:T(8,128)S(1)} %get-tuple-element.120.one), channel_id=1, source_target_pairs={{0,2},{1,3},{2,0},{3,1},{4,6},{5,7},{6,4},{7,5},{8,10},{9,11},{10,... | collective-permute-start | bytes 12296 | tf_op jit(solution)/shard_map/ppermute | solution.py:451
  22.5 1.1 collective-permute-start.8
  23.5 0.0 copy-done.2
  23.5 3.2 %transform.1.coeffs = f32[6144,128]{1,0:T(8,128)S(1)} custom-call(f32[6144,128]{1,0:T(8,128)S(1)} %get-tuple-element.78.curls, bf16[2048,256]{1,0:T(8,128)(2,1)S(1)} %copy-done.2), custom_call_target="tpu_custom_call" | custom-call | flops 805306368 | bytes 7500000 | tf_op jit(solution)/shard_map/transform/pallas_call | solution.py:259
  26.7 0.0 collective-permute-done.6.two
  26.7 0.0 collective-permute-done.7.three
  26.7 0.0 collective-permute-done.8.four
  26.7 5.0 %pack45.1 = f32[8704,128]{1,0:T(8,128)S(1)} custom-call(s32[16,128]{1,0:T(8,128)S(1)} %get-tuple-element.70.words, f32[6144,128]{1,0:T(8,128)S(1)} %transform.1.coeffs, f32[64,128]{1,0:T(8,128)S(1)} %get-tuple-element.119.head, f32[8,128]{1,0:T(8,128)S(1)} %get-tuple-element.120.one, f32[8,128]{1,0:T(8,128)S(1)} %collective-permute-done.6.two, ...), custom_call_target="tpu_custom_call" | custom-call | flops 200000000 | bytes 8000000 | tf_op jit(solution)/shard_map/pack45/pallas_call | solution.py:314
  31.8 112.4 %all_to_all.9 = f32[64,136,128]{2,1,0:T(8,128)S(1)} all-to-all(f32[64,136,128]{2,1,0:T(8,128)S(1)} %bitcast.11), channel_id=1, replica_groups=mesh['gx'=8,'gy'=8,'wa'=4] {'gx','gy'}, dimensions={0} | all-to-all | bytes 8912896 | tf_op jit(solution)/shard_map/all_to_all | solution.py:427
  144.1 10.4 %unpack45.1 = (f32[3,4096,128]{2,1,0:T(8,128)}, s32[1,1]{1,0:T(1,128)}, f32[64,128]{1,0:T(8,128)S(1)}) custom-call(f32[8704,128]{1,0:T(8,128)S(1)} %bitcast.10), custom_call_target="tpu_custom_call" | custom-call | flops 200000000 | bytes 11000000 | tf_op jit(solution)/shard_map/unpack45/pallas_call | solution.py:397
  154.5 0.8 while.9
Async XLA Ops:
  0.0 1.9 %copy-start.1 = (f32[3,32,64,128]{3,2,1,0:T(8,128)S(1)}, f32[3,32,64,128]{3,2,1,0:T(8,128)}, u32[]{:S(2)}) copy-start(f32[3,32,64,128]{3,2,1,0:T(8,128)} %param.6) | copy-start | bytes 9437188
  1.9 21.6 %copy-start.2 = (bf16[2048,256]{1,0:T(8,128)(2,1)S(1)}, bf16[2048,256]{1,0:T(8,128)(2,1)}, u32[]{:S(2)}) copy-start(bf16[2048,256]{1,0:T(8,128)(2,1)} %constant.8.clone.tables) | copy-start | bytes 3145732
  2.7 7.5 %collective-permute-start.4 = (f32[64,128]{1,0:T(8,128)S(1)}, f32[64,128]{1,0:T(8,128)S(1)}, u32[]{:S(2)}, u32[]{:S(2)}) collective-permute-start(f32[64,128]{1,0:T(8,128)S(1)} %get-tuple-element.76), channel_id=1, source_target_pairs={{0,1},{1,2},{2,3},{3,0},{4,5},{5,6},{6,7},{7,4},{8,9},{9,10},{10,1... | collective-permute-start | bytes 98312 | tf_op jit(solution)/shard_map/ppermute | solution.py:447
  4.9 11.6 %collective-permute-start.5 = (f32[64,128]{1,0:T(8,128)S(1)}, f32[64,128]{1,0:T(8,128)S(1)}, u32[]{:S(2)}, u32[]{:S(2)}) collective-permute-start(f32[64,128]{1,0:T(8,128)S(1)} %get-tuple-element.76), channel_id=1, source_target_pairs={{0,3},{1,0},{2,1},{3,2},{4,7},{5,4},{6,5},{7,6},{8,11},{9,8},{10,9... | collective-permute-start | bytes 98312 | tf_op jit(solution)/shard_map/ppermute | solution.py:447
  6.4 10.1 %collective-permute-start = (f32[128,128]{1,0:T(8,128)S(1)}, f32[128,128]{1,0:T(8,128)S(1)}, u32[]{:S(2)}, u32[]{:S(2)}) collective-permute-start(f32[128,128]{1,0:T(8,128)S(1)} %get-tuple-element.72), channel_id=1, source_target_pairs={{0,32},{32,64},{64,96},{96,128},{128,160},{160,192},{192,224},{224... | collective-permute-start | bytes 196616 | tf_op jit(solution)/shard_map/ppermute | solution.py:445
  8.6 7.9 %collective-permute-start.1 = (f32[128,128]{1,0:T(8,128)S(1)}, f32[128,128]{1,0:T(8,128)S(1)}, u32[]{:S(2)}, u32[]{:S(2)}) collective-permute-start(f32[128,128]{1,0:T(8,128)S(1)} %get-tuple-element.73), channel_id=1, source_target_pairs={{0,224},{32,0},{64,32},{96,64},{128,96},{160,128},{192,160},{224,1... | collective-permute-start | bytes 196616 | tf_op jit(solution)/shard_map/ppermute | solution.py:445
  9.2 7.3 %collective-permute-start.2 = (f32[64,128]{1,0:T(8,128)S(1)}, f32[64,128]{1,0:T(8,128)S(1)}, u32[]{:S(2)}, u32[]{:S(2)}) collective-permute-start(f32[64,128]{1,0:T(8,128)S(1)} %get-tuple-element.74), channel_id=1, source_target_pairs={{0,4},{4,8},{8,12},{12,16},{16,20},{20,24},{24,28},{28,0},{1,5},{5... | collective-permute-start | bytes 98312 | tf_op jit(solution)/shard_map/ppermute | solution.py:446
  10.2 6.3 %collective-permute-start.3 = (f32[64,128]{1,0:T(8,128)S(1)}, f32[64,128]{1,0:T(8,128)S(1)}, u32[]{:S(2)}, u32[]{:S(2)}) collective-permute-start(f32[64,128]{1,0:T(8,128)S(1)} %get-tuple-element.75), channel_id=1, source_target_pairs={{0,28},{4,0},{8,4},{12,8},{16,12},{20,16},{24,20},{28,24},{1,29},{... | collective-permute-start | bytes 98312 | tf_op jit(solution)/shard_map/ppermute | solution.py:446
  19.7 7.0 %collective-permute-start.6 = (f32[8,128]{1,0:T(8,128)S(1)}, f32[8,128]{1,0:T(8,128)S(1)}, u32[]{:S(2)}, u32[]{:S(2)}) collective-permute-start(f32[8,128]{1,0:T(8,128)S(1)} %get-tuple-element.120.one), channel_id=1, source_target_pairs={{0,1},{1,2},{2,3},{3,0},{4,5},{5,6},{6,7},{7,4},{8,9},{9,10},{10,1... | collective-permute-start | bytes 12296 | tf_op jit(solution)/shard_map/ppermute | solution.py:451
  19.8 6.9 %collective-permute-start.7 = (f32[8,128]{1,0:T(8,128)S(1)}, f32[8,128]{1,0:T(8,128)S(1)}, u32[]{:S(2)}, u32[]{:S(2)}) collective-permute-start(f32[8,128]{1,0:T(8,128)S(1)} %get-tuple-element.120.one), channel_id=1, source_target_pairs={{0,2},{1,3},{2,0},{3,1},{4,6},{5,7},{6,4},{7,5},{8,10},{9,11},{10,... | collective-permute-start | bytes 12296 | tf_op jit(solution)/shard_map/ppermute | solution.py:451
  22.5 4.3 %collective-permute-start.8 = (f32[8,128]{1,0:T(8,128)S(1)}, f32[8,128]{1,0:T(8,128)S(1)}, u32[]{:S(2)}, u32[]{:S(2)}) collective-permute-start(f32[8,128]{1,0:T(8,128)S(1)} %get-tuple-element.120.one), channel_id=1, source_target_pairs={{0,3},{1,0},{2,1},{3,2},{4,7},{5,4},{6,5},{7,6},{8,11},{9,8},{10,9... | collective-permute-start | bytes 12296 | tf_op jit(solution)/shard_map/ppermute | solution.py:451

commit v4 on v3

--- a/solution.py
+++ b/solution.py
@@ -7,6 +7,7 @@
 from jax.experimental import pallas as pl
 from jax.experimental.pallas import tpu as pltpu
 from jax.sharding import PartitionSpec as P
+
 
 BY = 8
 BZ = 16
@@ -88,7 +89,8 @@
     )(vel2)
 
 
-def index_kernel(mixed, words, wide, head):
+def index_kernel(mixed, ylo_in, yhi_in, zt_in, words, wide, head, ylo, yhi, zt):
+    ylo[...], yhi[...], zt[...] = ylo_in[...], yhi_in[...], zt_in[...]
     chunks = NBLK // LANES
     t = mixed[...] >> 8
     ln = mixed[...] & 255
@@ -129,7 +131,7 @@
     head[...] = jnp.where(lane < CAP, lens, jnp.where(lane == CAP + 1, spill, 0.0))
 
 
-def index(mixed):
+def index(mixed, *kept):
     i32 = jnp.int32
     return pl.pallas_call(
         index_kernel,
@@ -137,15 +139,16 @@
             jax.ShapeDtypeStruct((NBLK // LANES, LANES), i32),
             jax.ShapeDtypeStruct((NBLK // LANES, LANES), i32),
             jax.ShapeDtypeStruct((WRITERS, LANES), jnp.float32),
+            *[jax.ShapeDtypeStruct(k.shape, k.dtype) for k in kept],
         ],
         cost_estimate=pl.CostEstimate(flops=20_000_000, bytes_accessed=100_000, transcendentals=0),
         compiler_params=pltpu.CompilerParams(vmem_limit_bytes=8 << 20),
         name="index",
-    )(mixed)
-
-
-PLANES = 4
-PAIR = 2
+    )(mixed, *kept)
+
+
+PLANES = 8
+PAIR = 4
 
 
 def curl_kernel(vel, xprev, xnext, yprev, ynext, zprev, znext, head, curls, mine, ends):
@@ -324,7 +327,6 @@
             flops=200_000_000, bytes_accessed=8_000_000, transcendentals=0
         ),
         compiler_params=pltpu.CompilerParams(vmem_limit_bytes=22 << 20),
-        name=f"pack{rows}",
     )(words, coeffs, head, *sums)
 
 
@@ -419,7 +421,6 @@
             flops=200_000_000, bytes_accessed=11_000_000, transcendentals=0
         ),
         compiler_params=pltpu.CompilerParams(vmem_limit_bytes=24 << 20),
-        name=f"unpack{rows}",
     )(*args)
 
 
@@ -429,10 +430,9 @@
     )
 
 
-def local(velocity, lengths, destinations):
+def body_of(velocity, lengths, destinations):
     vel2 = velocity.reshape(COMP * CX * CY, LANES)
-    targets = destinations.reshape(NBLK // LANES, LANES)
-    lens = lengths.reshape(NBLK // LANES, LANES)
+    mixed = (destinations * 256 + lengths.reshape(destinations.shape)).reshape(NBLK // LANES, LANES)
 
     xlo, xhi, ylo, yhi, zt, vel2 = faces(vel2)
 
@@ -443,9 +443,9 @@
 
     n_x, n_y, n_z = (lax.axis_size(a) for a in ("gx", "gy", "wa"))
     xprev, xnext = ring("gx", n_x, 1)(xhi), ring("gx", n_x, -1)(xlo)
+    words, wide, head, ylo, yhi, zt = index(mixed, ylo, yhi, zt)
     yprev, ynext = ring("gy", n_y, 1)(yhi), ring("gy", n_y, -1)(ylo)
     zprev, znext = ring("wa", n_z, 1)(zt), ring("wa", n_z, -1)(zt)
-    words, wide, head = index(targets * 256 + lens)
 
     curls, mine = curl_of(vel2, xprev, xnext, yprev, ynext, zprev, znext, head)
     sums = [mine] + [ring("wa", n_z, d)(mine) for d in range(1, n_z)]
@@ -465,7 +465,7 @@
 
 def solution(mesh):
     return jax.shard_map(
-        local,
+        body_of,
         mesh=mesh,
         in_specs=(
             P(None, "gx", "gy", "wa"),

time: 156 us -> 156 us (level)
  blocking collectives: 112 us -> 114 us
  transfers between devices with their start and end apart: 9 -> 9, of which waited for: 0 -> 1; matrix products, arithmetic and copies ran while one was open for 1% -> 0% of each run, Pallas kernels for 3% -> 2%
where the time goes in v4:
time: 156 us
  blocking collectives  114 us (73%)
  Pallas kernels  21.8 us (14%)
  starting transfers between devices  15 us (10%)
  local copies, waits for them, and re-layouts  1.89 us (1%)
    all_to_all x1, blocking collectives, exchange(): lax.all_to_all(buffer.reshape(WRITERS, span_of(rows), LANES), G, 0, 0, ti...  114 us
    pallas_call x1, Pallas kernels, unpack(): pl.pallas_call(functools.partial(unpack_kernel, rows), grid=(WRITERS // S...  10.4 us
    pallas_call x1, Pallas kernels, pack(): pl.pallas_call(functools.partial(pack_kernel, rows), in_specs=[pl.BlockSp...  5.02 us
    ppermute x2, starting transfers between devices, body_of(): yprev, ynext = (ring('gy', n_y, 1)(yhi), ring('gy', n_y, -1)(ylo))  4.97 us
    ppermute x2, starting transfers between devices, body_of(): zprev, znext = (ring('wa', n_z, 1)(zt), ring('wa', n_z, -1)(zt))  4.14 us
    ppermute x3, starting transfers between devices, body_of(): sums = [mine] + [ring('wa', n_z, d)(mine) for d in range(1, n_z)]  3.85 us
  transfers between devices with their start and end apart: 9, of which 1 were waited for; matrix products, arithmetic and copies ran while one was open for 0% of the time, Pallas kernels for 2%

profile of v4, /device:TPU:1, one launch (start us, length us, event | category | flops | bytes accessed | tf_op | source)
XLA Modules:
  0.0 155.6 jit_solution(512542503148677500)
XLA Ops:
  0.0 0.0 copy-start.1
  0.0 1.9 %copy-done.1 = f32[3,32,64,128]{3,2,1,0:T(8,128)S(1)} copy-done((f32[3,32,64,128]{3,2,1,0:T(8,128)S(1)}, f32[3,32,64,128]{3,2,1,0:T(8,128)}, u32[]{:S(2)}) %copy-start.1) | copy-done | bytes 3145752
  1.9 0.0 copy-start.2
  1.9 0.8 faces.1
  2.7 0.7 bitcast_add_fusion
  3.4 0.8 index.1
  4.2 2.2 %collective-permute-start.4 = (f32[64,128]{1,0:T(8,128)S(1)}, f32[64,128]{1,0:T(8,128)S(1)}, u32[]{:S(2)}, u32[]{:S(2)}) collective-permute-start(f32[64,128]{1,0:T(8,128)S(1)} %get-tuple-element.82), channel_id=1, source_target_pairs={{0,1},{1,2},{2,3},{3,0},{4,5},{5,6},{6,7},{7,4},{8,9},{9,10},{10,1... | collective-permute-start | bytes 98312 | tf_op jit(solution)/shard_map/ppermute | solution.py:448
  6.4 2.1 %collective-permute-start = (f32[128,128]{1,0:T(8,128)S(1)}, f32[128,128]{1,0:T(8,128)S(1)}, u32[]{:S(2)}, u32[]{:S(2)}) collective-permute-start(f32[128,128]{1,0:T(8,128)S(1)} %get-tuple-element.78), channel_id=1, source_target_pairs={{0,32},{32,64},{64,96},{96,128},{128,160},{160,192},{192,224},{224... | collective-permute-start | bytes 196616 | tf_op jit(solution)/shard_map/ppermute | solution.py:445
  8.4 0.0 collective-permute-start.1
  8.4 2.0 %collective-permute-start.5 = (f32[64,128]{1,0:T(8,128)S(1)}, f32[64,128]{1,0:T(8,128)S(1)}, u32[]{:S(2)}, u32[]{:S(2)}) collective-permute-start(f32[64,128]{1,0:T(8,128)S(1)} %get-tuple-element.82), channel_id=1, source_target_pairs={{0,3},{1,0},{2,1},{3,2},{4,7},{5,4},{6,5},{7,6},{8,11},{9,8},{10,9... | collective-permute-start | bytes 98312 | tf_op jit(solution)/shard_map/ppermute | solution.py:448
  10.4 1.0 collective-permute-start.2
  11.4 0.0 collective-permute-done.4.zprev
  11.5 3.9 %collective-permute-start.3 = (f32[64,128]{1,0:T(8,128)S(1)}, f32[64,128]{1,0:T(8,128)S(1)}, u32[]{:S(2)}, u32[]{:S(2)}) collective-permute-start(f32[64,128]{1,0:T(8,128)S(1)} %get-tuple-element.81), channel_id=1, source_target_pairs={{0,28},{4,0},{8,4},{12,8},{16,12},{20,16},{24,20},{28,24},{1,29},{... | collective-permute-start | bytes 98312 | tf_op jit(solution)/shard_map/ppermute | solution.py:447
  15.4 0.0 collective-permute-done.5.znext
  15.4 1.3 collective-permute-done.2.yprev
  16.7 0.0 collective-permute-done.3.ynext
  16.7 0.0 collective-permute-done.xprev
  16.7 0.0 collective-permute-done.1.xnext
  16.7 2.5 %curl.1 = (f32[6144,128]{1,0:T(8,128)S(1)}, f32[8,128]{1,0:T(8,128)S(1)}) custom-call(f32[6144,128]{1,0:T(8,128)S(1)} %get-tuple-element.77.vel, f32[128,128]{1,0:T(8,128)S(1)} %collective-permute-done.xprev, f32[128,128]{1,0:T(8,128)S(1)} %collective-permute-done.1.xnext, f32[64,128]{1,0:T(8,128)S(1)} %collective-permute-done.2.yprev, ...), custom_call_target="tpu_custom_call" | custom-call | flops 40000000 | bytes 7500000 | tf_op jit(solution)/shard_map/curl/pallas_call | solution.py:209
  19.2 0.2 collective-permute-start.6
  19.4 2.6 %collective-permute-start.7 = (f32[8,128]{1,0:T(8,128)S(1)}, f32[8,128]{1,0:T(8,128)S(1)}, u32[]{:S(2)}, u32[]{:S(2)}) collective-permute-start(f32[8,128]{1,0:T(8,128)S(1)} %get-tuple-element.126.one), channel_id=1, source_target_pairs={{0,2},{1,3},{2,0},{3,1},{4,6},{5,7},{6,4},{7,5},{8,10},{9,11},{10,... | collective-permute-start | bytes 12296 | tf_op jit(solution)/shard_map/ppermute | solution.py:451
  22.0 1.1 collective-permute-start.8
  23.1 0.0 copy-done.2
  23.1 2.4 %transform.1.coeffs = f32[6144,128]{1,0:T(8,128)S(1)} custom-call(f32[6144,128]{1,0:T(8,128)S(1)} %get-tuple-element.84.curls, bf16[2048,256]{1,0:T(8,128)(2,1)S(1)} %copy-done.2), custom_call_target="tpu_custom_call" | custom-call | flops 805306368 | bytes 7500000 | tf_op jit(solution)/shard_map/transform/pallas_call | solution.py:262
  25.4 0.0 collective-permute-done.6.two
  25.5 0.0 collective-permute-done.7.three
  25.5 0.0 collective-permute-done.8.four
  25.5 5.0 %shard_map.46 = f32[8704,128]{1,0:T(8,128)S(1)} custom-call(s32[16,128]{1,0:T(8,128)S(1)} %get-tuple-element.76.words, f32[6144,128]{1,0:T(8,128)S(1)} %transform.1.coeffs, f32[64,128]{1,0:T(8,128)S(1)} %get-tuple-element.125.head, f32[8,128]{1,0:T(8,128)S(1)} %get-tuple-element.126.one, f32[8,128]{1,0:T(8,128)S(1)} %collective-permute-done.6.two, ...), custom_call_target="tpu_custom_call" | custom-call | flops 200000000 | bytes 8000000 | tf_op jit(solution)/shard_map/pallas_call | solution.py:317
  30.5 113.7 %all_to_all.9 = f32[64,136,128]{2,1,0:T(8,128)S(1)} all-to-all(f32[64,136,128]{2,1,0:T(8,128)S(1)} %bitcast.12), channel_id=1, replica_groups=mesh['gx'=8,'gy'=8,'wa'=4] {'gx','gy'}, dimensions={0} | all-to-all | bytes 8912896 | tf_op jit(solution)/shard_map/all_to_all | solution.py:428
  144.2 10.4 %shard_map.47 = (f32[3,4096,128]{2,1,0:T(8,128)}, s32[1,1]{1,0:T(1,128)}, f32[64,128]{1,0:T(8,128)S(1)}) custom-call(f32[8704,128]{1,0:T(8,128)S(1)} %bitcast.11), custom_call_target="tpu_custom_call" | custom-call | flops 200000000 | bytes 11000000 | tf_op jit(solution)/shard_map/pallas_call | solution.py:399
  154.6 0.8 while.9
Async XLA Ops:
  0.0 1.9 %copy-start.1 = (f32[3,32,64,128]{3,2,1,0:T(8,128)S(1)}, f32[3,32,64,128]{3,2,1,0:T(8,128)}, u32[]{:S(2)}) copy-start(f32[3,32,64,128]{3,2,1,0:T(8,128)} %param.6) | copy-start | bytes 9437188
  1.9 21.2 %copy-start.2 = (bf16[2048,256]{1,0:T(8,128)(2,1)S(1)}, bf16[2048,256]{1,0:T(8,128)(2,1)}, u32[]{:S(2)}) copy-start(bf16[2048,256]{1,0:T(8,128)(2,1)} %constant.8.clone.tables) | copy-start | bytes 3145732
  4.2 7.2 %collective-permute-start.4 = (f32[64,128]{1,0:T(8,128)S(1)}, f32[64,128]{1,0:T(8,128)S(1)}, u32[]{:S(2)}, u32[]{:S(2)}) collective-permute-start(f32[64,128]{1,0:T(8,128)S(1)} %get-tuple-element.82), channel_id=1, source_target_pairs={{0,1},{1,2},{2,3},{3,0},{4,5},{5,6},{6,7},{7,4},{8,9},{9,10},{10,1... | collective-permute-start | bytes 98312 | tf_op jit(solution)/shard_map/ppermute | solution.py:448
  6.4 10.3 %collective-permute-start = (f32[128,128]{1,0:T(8,128)S(1)}, f32[128,128]{1,0:T(8,128)S(1)}, u32[]{:S(2)}, u32[]{:S(2)}) collective-permute-start(f32[128,128]{1,0:T(8,128)S(1)} %get-tuple-element.78), channel_id=1, source_target_pairs={{0,32},{32,64},{64,96},{96,128},{128,160},{160,192},{192,224},{224... | collective-permute-start | bytes 196616 | tf_op jit(solution)/shard_map/ppermute | solution.py:445
  8.4 8.3 %collective-permute-start.1 = (f32[128,128]{1,0:T(8,128)S(1)}, f32[128,128]{1,0:T(8,128)S(1)}, u32[]{:S(2)}, u32[]{:S(2)}) collective-permute-start(f32[128,128]{1,0:T(8,128)S(1)} %get-tuple-element.79), channel_id=1, source_target_pairs={{0,224},{32,0},{64,32},{96,64},{128,96},{160,128},{192,160},{224,1... | collective-permute-start | bytes 196616 | tf_op jit(solution)/shard_map/ppermute | solution.py:445
  8.4 7.0 %collective-permute-start.5 = (f32[64,128]{1,0:T(8,128)S(1)}, f32[64,128]{1,0:T(8,128)S(1)}, u32[]{:S(2)}, u32[]{:S(2)}) collective-permute-start(f32[64,128]{1,0:T(8,128)S(1)} %get-tuple-element.82), channel_id=1, source_target_pairs={{0,3},{1,0},{2,1},{3,2},{4,7},{5,4},{6,5},{7,6},{8,11},{9,8},{10,9... | collective-permute-start | bytes 98312 | tf_op jit(solution)/shard_map/ppermute | solution.py:448
  10.4 6.3 %collective-permute-start.2 = (f32[64,128]{1,0:T(8,128)S(1)}, f32[64,128]{1,0:T(8,128)S(1)}, u32[]{:S(2)}, u32[]{:S(2)}) collective-permute-start(f32[64,128]{1,0:T(8,128)S(1)} %get-tuple-element.80), channel_id=1, source_target_pairs={{0,4},{4,8},{8,12},{12,16},{16,20},{20,24},{24,28},{28,0},{1,5},{5... | collective-permute-start | bytes 98312 | tf_op jit(solution)/shard_map/ppermute | solution.py:447
  11.5 5.2 %collective-permute-start.3 = (f32[64,128]{1,0:T(8,128)S(1)}, f32[64,128]{1,0:T(8,128)S(1)}, u32[]{:S(2)}, u32[]{:S(2)}) collective-permute-start(f32[64,128]{1,0:T(8,128)S(1)} %get-tuple-element.81), channel_id=1, source_target_pairs={{0,28},{4,0},{8,4},{12,8},{16,12},{20,16},{24,20},{28,24},{1,29},{... | collective-permute-start | bytes 98312 | tf_op jit(solution)/shard_map/ppermute | solution.py:447
  19.2 6.2 %collective-permute-start.6 = (f32[8,128]{1,0:T(8,128)S(1)}, f32[8,128]{1,0:T(8,128)S(1)}, u32[]{:S(2)}, u32[]{:S(2)}) collective-permute-start(f32[8,128]{1,0:T(8,128)S(1)} %get-tuple-element.126.one), channel_id=1, source_target_pairs={{0,1},{1,2},{2,3},{3,0},{4,5},{5,6},{6,7},{7,4},{8,9},{9,10},{10,1... | collective-permute-start | bytes 12296 | tf_op jit(solution)/shard_map/ppermute | solution.py:451
  19.4 6.1 %collective-permute-start.7 = (f32[8,128]{1,0:T(8,128)S(1)}, f32[8,128]{1,0:T(8,128)S(1)}, u32[]{:S(2)}, u32[]{:S(2)}) collective-permute-start(f32[8,128]{1,0:T(8,128)S(1)} %get-tuple-element.126.one), channel_id=1, source_target_pairs={{0,2},{1,3},{2,0},{3,1},{4,6},{5,7},{6,4},{7,5},{8,10},{9,11},{10,... | collective-permute-start | bytes 12296 | tf_op jit(solution)/shard_map/ppermute | solution.py:451
  22.0 3.5 %collective-permute-start.8 = (f32[8,128]{1,0:T(8,128)S(1)}, f32[8,128]{1,0:T(8,128)S(1)}, u32[]{:S(2)}, u32[]{:S(2)}) collective-permute-start(f32[8,128]{1,0:T(8,128)S(1)} %get-tuple-element.126.one), channel_id=1, source_target_pairs={{0,3},{1,0},{2,1},{3,2},{4,7},{5,4},{6,5},{7,6},{8,11},{9,8},{10,9... | collective-permute-start | bytes 12296 | tf_op jit(solution)/shard_map/ppermute | solution.py:451

commit v5 on v3

--- a/solution.py
+++ b/solution.py
@@ -144,8 +144,8 @@
     )(mixed)
 
 
-PLANES = 4
-PAIR = 2
+PLANES = 32
+PAIR = 16
 
 
 def curl_kernel(vel, xprev, xnext, yprev, ynext, zprev, znext, head, curls, mine, ends):
@@ -268,7 +268,7 @@
     )(curls, tables)
 
 
-WIDTH = 2
+WIDTH = 4
 
 
 def pack_kernel(rows, words, coeffs, head, one, two, three, four, out, room):
@@ -291,12 +291,13 @@
     lax.fori_loop(0, NBLK // LANES // WIDTH, body, 0)
 
     def settle(w, carry):
-        source = pl.multiple_of(w * local_span, 8)
-        target = pl.multiple_of(w * span, 8)
-        out[pl.ds(target, span)] = room[pl.ds(source, span)]
+        for k in range(8):
+            source = pl.multiple_of((w * 8 + k) * local_span, 8)
+            target = pl.multiple_of((w * 8 + k) * span, 8)
+            out[pl.ds(target, span)] = room[pl.ds(source, span)]
         return carry
 
-    lax.fori_loop(0, WRITERS, settle, 0)
+    lax.fori_loop(0, WRITERS // 8, settle, 0)
     small = iota((8, LANES), 1)
     both = jnp.where(
         small == CAP,
@@ -431,8 +432,7 @@
 
 def local(velocity, lengths, destinations):
     vel2 = velocity.reshape(COMP * CX * CY, LANES)
-    targets = destinations.reshape(NBLK // LANES, LANES)
-    lens = lengths.reshape(NBLK // LANES, LANES)
+    mixed = (destinations * 256 + lengths.reshape(destinations.shape)).reshape(NBLK // LANES, LANES)
 
     xlo, xhi, ylo, yhi, zt, vel2 = faces(vel2)
 
@@ -445,7 +445,7 @@
     xprev, xnext = ring("gx", n_x, 1)(xhi), ring("gx", n_x, -1)(xlo)
     yprev, ynext = ring("gy", n_y, 1)(yhi), ring("gy", n_y, -1)(ylo)
     zprev, znext = ring("wa", n_z, 1)(zt), ring("wa", n_z, -1)(zt)
-    words, wide, head = index(targets * 256 + lens)
+    words, wide, head = index(mixed)
 
     curls, mine = curl_of(vel2, xprev, xnext, yprev, ynext, zprev, znext, head)
     sums = [mine] + [ring("wa", n_z, d)(mine) for d in range(1, n_z)]

time: 156 us -> 153 us (0.981)
  Pallas kernels: 23.3 us -> 20.2 us
  blocking collectives: 112 us -> 114 us
    pallas_call x1, Pallas kernels: 3.16 us -> 1.54 us  [transform_of(): pl.pallas_call(transform_kernel, out_shape=jax.ShapeDtypeStruct((rows, LA...]
  transfers between devices with their start and end apart: 9 -> 9, of which waited for: 0 -> 0; matrix products, arithmetic and copies ran while one was open for 1% -> 0% of each run, Pallas kernels for 3% -> 2%
where the time goes in v5:
time: 153 us
  blocking collectives  114 us (75%)
  Pallas kernels  20.2 us (13%)
  starting transfers between devices  15.4 us (10%)
  local copies, waits for them, and re-layouts  1.89 us (1%)
    all_to_all x1, blocking collectives, exchange(): lax.all_to_all(buffer.reshape(WRITERS, span_of(rows), LANES), G, 0, 0, ti...  114 us
    pallas_call x1, Pallas kernels, unpack(): pl.pallas_call(functools.partial(unpack_kernel, rows), grid=(WRITERS // S...  10.4 us
    ppermute x2, starting transfers between devices, local(): yprev, ynext = (ring('gy', n_y, 1)(yhi), ring('gy', n_y, -1)(ylo))  5.05 us
    pallas_call x1, Pallas kernels, pack(): pl.pallas_call(functools.partial(pack_kernel, rows), in_specs=[pl.BlockSp...  4.69 us
    ppermute x3, starting transfers between devices, local(): sums = [mine] + [ring('wa', n_z, d)(mine) for d in range(1, n_z)]  3.85 us
    ppermute x2, starting transfers between devices, local(): zprev, znext = (ring('wa', n_z, 1)(zt), ring('wa', n_z, -1)(zt))  3.72 us
  transfers between devices with their start and end apart: 9, of which 0 were waited for; matrix products, arithmetic and copies ran while one was open for 0% of the time, Pallas kernels for 2%

profile of v5, /device:TPU:1, one launch (start us, length us, event | category | flops | bytes accessed | tf_op | source)
XLA Modules:
  0.0 152.9 jit_solution(8643693042053887299)
XLA Ops:
  0.0 0.0 copy-start.1
  0.0 1.9 %copy-done.1 = f32[3,32,64,128]{3,2,1,0:T(8,128)S(1)} copy-done((f32[3,32,64,128]{3,2,1,0:T(8,128)S(1)}, f32[3,32,64,128]{3,2,1,0:T(8,128)}, u32[]{:S(2)}) %copy-start.1) | copy-done | bytes 3145752
  1.9 0.0 copy-start.2
  1.9 0.8 faces.1
  2.7 2.2 %collective-permute-start.4 = (f32[64,128]{1,0:T(8,128)S(1)}, f32[64,128]{1,0:T(8,128)S(1)}, u32[]{:S(2)}, u32[]{:S(2)}) collective-permute-start(f32[64,128]{1,0:T(8,128)S(1)} %get-tuple-element.76), channel_id=1, source_target_pairs={{0,1},{1,2},{2,3},{3,0},{4,5},{5,6},{6,7},{7,4},{8,9},{9,10},{10,1... | collective-permute-start | bytes 98312 | tf_op jit(solution)/shard_map/ppermute | solution.py:447
  4.9 1.5 collective-permute-start.5
  6.4 2.2 %collective-permute-start = (f32[128,128]{1,0:T(8,128)S(1)}, f32[128,128]{1,0:T(8,128)S(1)}, u32[]{:S(2)}, u32[]{:S(2)}) collective-permute-start(f32[128,128]{1,0:T(8,128)S(1)} %get-tuple-element.72), channel_id=1, source_target_pairs={{0,32},{32,64},{64,96},{96,128},{128,160},{160,192},{192,224},{224... | collective-permute-start | bytes 196616 | tf_op jit(solution)/shard_map/ppermute | solution.py:445
  8.6 0.6 collective-permute-start.1
  9.2 1.0 collective-permute-start.2
  10.2 0.0 collective-permute-done.4.zprev
  10.2 4.0 %collective-permute-start.3 = (f32[64,128]{1,0:T(8,128)S(1)}, f32[64,128]{1,0:T(8,128)S(1)}, u32[]{:S(2)}, u32[]{:S(2)}) collective-permute-start(f32[64,128]{1,0:T(8,128)S(1)} %get-tuple-element.75), channel_id=1, source_target_pairs={{0,28},{4,0},{8,4},{12,8},{16,12},{20,16},{24,20},{28,24},{1,29},{... | collective-permute-start | bytes 98312 | tf_op jit(solution)/shard_map/ppermute | solution.py:446
  14.2 0.7 bitcast_add_fusion
  15.0 0.8 index.1
  15.8 0.0 collective-permute-done.5.znext
  15.8 0.0 collective-permute-done.2.yprev
  15.8 0.0 collective-permute-done.3.ynext
  15.8 0.0 collective-permute-done.xprev
  15.8 0.0 collective-permute-done.1.xnext
  15.9 2.0 %curl.1 = (f32[6144,128]{1,0:T(8,128)S(1)}, f32[8,128]{1,0:T(8,128)S(1)}) custom-call(f32[6144,128]{1,0:T(8,128)S(1)} %get-tuple-element.71.vel, f32[128,128]{1,0:T(8,128)S(1)} %collective-permute-done.xprev, f32[128,128]{1,0:T(8,128)S(1)} %collective-permute-done.1.xnext, f32[64,128]{1,0:T(8,128)S(1)} %collective-permute-done.2.yprev, ...), custom_call_target="tpu_custom_call" | custom-call | flops 40000000 | bytes 7500000 | tf_op jit(solution)/shard_map/curl/pallas_call | solution.py:206
  17.9 0.2 collective-permute-start.6
  18.0 2.6 %collective-permute-start.7 = (f32[8,128]{1,0:T(8,128)S(1)}, f32[8,128]{1,0:T(8,128)S(1)}, u32[]{:S(2)}, u32[]{:S(2)}) collective-permute-start(f32[8,128]{1,0:T(8,128)S(1)} %get-tuple-element.120.one), channel_id=1, source_target_pairs={{0,2},{1,3},{2,0},{3,1},{4,6},{5,7},{6,4},{7,5},{8,10},{9,11},{10,... | collective-permute-start | bytes 12296 | tf_op jit(solution)/shard_map/ppermute | solution.py:451
  20.7 1.1 collective-permute-start.8
  21.7 0.0 copy-done.2
  21.7 1.5 %transform.1.coeffs = f32[6144,128]{1,0:T(8,128)S(1)} custom-call(f32[6144,128]{1,0:T(8,128)S(1)} %get-tuple-element.78.curls, bf16[2048,256]{1,0:T(8,128)(2,1)S(1)} %copy-done.2), custom_call_target="tpu_custom_call" | custom-call | flops 805306368 | bytes 7500000 | tf_op jit(solution)/shard_map/transform/pallas_call | solution.py:259
  23.3 0.0 collective-permute-done.6.two
  23.3 0.0 collective-permute-done.7.three
  23.3 0.0 collective-permute-done.8.four
  23.3 4.7 %pack45.1 = f32[8704,128]{1,0:T(8,128)S(1)} custom-call(s32[16,128]{1,0:T(8,128)S(1)} %get-tuple-element.70.words, f32[6144,128]{1,0:T(8,128)S(1)} %transform.1.coeffs, f32[64,128]{1,0:T(8,128)S(1)} %get-tuple-element.119.head, f32[8,128]{1,0:T(8,128)S(1)} %get-tuple-element.120.one, f32[8,128]{1,0:T(8,128)S(1)} %collective-permute-done.6.two, ...), custom_call_target="tpu_custom_call" | custom-call | flops 200000000 | bytes 8000000 | tf_op jit(solution)/shard_map/pack45/pallas_call | solution.py:315
  28.0 113.7 %all_to_all.9 = f32[64,136,128]{2,1,0:T(8,128)S(1)} all-to-all(f32[64,136,128]{2,1,0:T(8,128)S(1)} %bitcast.12), channel_id=1, replica_groups=mesh['gx'=8,'gy'=8,'wa'=4] {'gx','gy'}, dimensions={0} | all-to-all | bytes 8912896 | tf_op jit(solution)/shard_map/all_to_all | solution.py:428
  141.7 10.4 %unpack45.1 = (f32[3,4096,128]{2,1,0:T(8,128)}, s32[1,1]{1,0:T(1,128)}, f32[64,128]{1,0:T(8,128)S(1)}) custom-call(f32[8704,128]{1,0:T(8,128)S(1)} %bitcast.11), custom_call_target="tpu_custom_call" | custom-call | flops 200000000 | bytes 11000000 | tf_op jit(solution)/shard_map/unpack45/pallas_call | solution.py:398
  152.1 0.6 while.9
Async XLA Ops:
  0.0 1.9 %copy-start.1 = (f32[3,32,64,128]{3,2,1,0:T(8,128)S(1)}, f32[3,32,64,128]{3,2,1,0:T(8,128)}, u32[]{:S(2)}) copy-start(f32[3,32,64,128]{3,2,1,0:T(8,128)} %param.6) | copy-start | bytes 9437188
  1.9 19.8 %copy-start.2 = (bf16[2048,256]{1,0:T(8,128)(2,1)S(1)}, bf16[2048,256]{1,0:T(8,128)(2,1)}, u32[]{:S(2)}) copy-start(bf16[2048,256]{1,0:T(8,128)(2,1)} %constant.8.clone.tables) | copy-start | bytes 3145732
  2.7 7.5 %collective-permute-start.4 = (f32[64,128]{1,0:T(8,128)S(1)}, f32[64,128]{1,0:T(8,128)S(1)}, u32[]{:S(2)}, u32[]{:S(2)}) collective-permute-start(f32[64,128]{1,0:T(8,128)S(1)} %get-tuple-element.76), channel_id=1, source_target_pairs={{0,1},{1,2},{2,3},{3,0},{4,5},{5,6},{6,7},{7,4},{8,9},{9,10},{10,1... | collective-permute-start | bytes 98312 | tf_op jit(solution)/shard_map/ppermute | solution.py:447
  4.9 10.9 %collective-permute-start.5 = (f32[64,128]{1,0:T(8,128)S(1)}, f32[64,128]{1,0:T(8,128)S(1)}, u32[]{:S(2)}, u32[]{:S(2)}) collective-permute-start(f32[64,128]{1,0:T(8,128)S(1)} %get-tuple-element.76), channel_id=1, source_target_pairs={{0,3},{1,0},{2,1},{3,2},{4,7},{5,4},{6,5},{7,6},{8,11},{9,8},{10,9... | collective-permute-start | bytes 98312 | tf_op jit(solution)/shard_map/ppermute | solution.py:447
  6.4 9.4 %collective-permute-start = (f32[128,128]{1,0:T(8,128)S(1)}, f32[128,128]{1,0:T(8,128)S(1)}, u32[]{:S(2)}, u32[]{:S(2)}) collective-permute-start(f32[128,128]{1,0:T(8,128)S(1)} %get-tuple-element.72), channel_id=1, source_target_pairs={{0,32},{32,64},{64,96},{96,128},{128,160},{160,192},{192,224},{224... | collective-permute-start | bytes 196616 | tf_op jit(solution)/shard_map/ppermute | solution.py:445
  8.6 7.3 %collective-permute-start.1 = (f32[128,128]{1,0:T(8,128)S(1)}, f32[128,128]{1,0:T(8,128)S(1)}, u32[]{:S(2)}, u32[]{:S(2)}) collective-permute-start(f32[128,128]{1,0:T(8,128)S(1)} %get-tuple-element.73), channel_id=1, source_target_pairs={{0,224},{32,0},{64,32},{96,64},{128,96},{160,128},{192,160},{224,1... | collective-permute-start | bytes 196616 | tf_op jit(solution)/shard_map/ppermute | solution.py:445
  9.2 6.6 %collective-permute-start.2 = (f32[64,128]{1,0:T(8,128)S(1)}, f32[64,128]{1,0:T(8,128)S(1)}, u32[]{:S(2)}, u32[]{:S(2)}) collective-permute-start(f32[64,128]{1,0:T(8,128)S(1)} %get-tuple-element.74), channel_id=1, source_target_pairs={{0,4},{4,8},{8,12},{12,16},{16,20},{20,24},{24,28},{28,0},{1,5},{5... | collective-permute-start | bytes 98312 | tf_op jit(solution)/shard_map/ppermute | solution.py:446
  10.2 5.6 %collective-permute-start.3 = (f32[64,128]{1,0:T(8,128)S(1)}, f32[64,128]{1,0:T(8,128)S(1)}, u32[]{:S(2)}, u32[]{:S(2)}) collective-permute-start(f32[64,128]{1,0:T(8,128)S(1)} %get-tuple-element.75), channel_id=1, source_target_pairs={{0,28},{4,0},{8,4},{12,8},{16,12},{20,16},{24,20},{28,24},{1,29},{... | collective-permute-start | bytes 98312 | tf_op jit(solution)/shard_map/ppermute | solution.py:446
  17.9 5.4 %collective-permute-start.6 = (f32[8,128]{1,0:T(8,128)S(1)}, f32[8,128]{1,0:T(8,128)S(1)}, u32[]{:S(2)}, u32[]{:S(2)}) collective-permute-start(f32[8,128]{1,0:T(8,128)S(1)} %get-tuple-element.120.one), channel_id=1, source_target_pairs={{0,1},{1,2},{2,3},{3,0},{4,5},{5,6},{6,7},{7,4},{8,9},{9,10},{10,1... | collective-permute-start | bytes 12296 | tf_op jit(solution)/shard_map/ppermute | solution.py:451
  18.0 5.2 %collective-permute-start.7 = (f32[8,128]{1,0:T(8,128)S(1)}, f32[8,128]{1,0:T(8,128)S(1)}, u32[]{:S(2)}, u32[]{:S(2)}) collective-permute-start(f32[8,128]{1,0:T(8,128)S(1)} %get-tuple-element.120.one), channel_id=1, source_target_pairs={{0,2},{1,3},{2,0},{3,1},{4,6},{5,7},{6,4},{7,5},{8,10},{9,11},{10,... | collective-permute-start | bytes 12296 | tf_op jit(solution)/shard_map/ppermute | solution.py:451
  20.7 2.6 %collective-permute-start.8 = (f32[8,128]{1,0:T(8,128)S(1)}, f32[8,128]{1,0:T(8,128)S(1)}, u32[]{:S(2)}, u32[]{:S(2)}) collective-permute-start(f32[8,128]{1,0:T(8,128)S(1)} %get-tuple-element.120.one), channel_id=1, source_target_pairs={{0,3},{1,0},{2,1},{3,2},{4,7},{5,4},{6,5},{7,6},{8,11},{9,8},{10,9... | collective-permute-start | bytes 12296 | tf_op jit(solution)/shard_map/ppermute | solution.py:451

commit v6 on v5

--- a/solution.py
+++ b/solution.py
@@ -145,7 +145,7 @@
 
 
 PLANES = 32
-PAIR = 16
+PAIR = 32
 
 
 def curl_kernel(vel, xprev, xnext, yprev, ynext, zprev, znext, head, curls, mine, ends):

time: 153 us -> 153 us (level)
  no operation moved by 1% of the time
where the time goes in v6:
time: 153 us
  blocking collectives  114 us (75%)
  Pallas kernels  20.1 us (13%)
  starting transfers between devices  15.4 us (10%)
  local copies, waits for them, and re-layouts  1.89 us (1%)
    all_to_all x1, blocking collectives, exchange(): lax.all_to_all(buffer.reshape(WRITERS, span_of(rows), LANES), G, 0, 0, ti...  114 us
    pallas_call x1, Pallas kernels, unpack(): pl.pallas_call(functools.partial(unpack_kernel, rows), grid=(WRITERS // S...  10.4 us
    ppermute x2, starting transfers between devices, local(): yprev, ynext = (ring('gy', n_y, 1)(yhi), ring('gy', n_y, -1)(ylo))  5.05 us
    pallas_call x1, Pallas kernels, pack(): pl.pallas_call(functools.partial(pack_kernel, rows), in_specs=[pl.BlockSp...  4.69 us
    ppermute x3, starting transfers between devices, local(): sums = [mine] + [ring('wa', n_z, d)(mine) for d in range(1, n_z)]  3.85 us
    ppermute x2, starting transfers between devices, local(): zprev, znext = (ring('wa', n_z, 1)(zt), ring('wa', n_z, -1)(zt))  3.72 us
  transfers between devices with their start and end apart: 9, of which 0 were waited for; matrix products, arithmetic and copies ran while one was open for 0% of the time, Pallas kernels for 2%

profile of v6, /device:TPU:1, one launch (start us, length us, event | category | flops | bytes accessed | tf_op | source)
XLA Modules:
  0.0 152.8 jit_solution(17374124416804512682)
XLA Ops:
  0.0 0.0 copy-start.1
  0.0 1.9 %copy-done.1 = f32[3,32,64,128]{3,2,1,0:T(8,128)S(1)} copy-done((f32[3,32,64,128]{3,2,1,0:T(8,128)S(1)}, f32[3,32,64,128]{3,2,1,0:T(8,128)}, u32[]{:S(2)}) %copy-start.1) | copy-done | bytes 3145752
  1.9 0.0 copy-start.2
  1.9 0.8 faces.1
  2.7 2.2 %collective-permute-start.4 = (f32[64,128]{1,0:T(8,128)S(1)}, f32[64,128]{1,0:T(8,128)S(1)}, u32[]{:S(2)}, u32[]{:S(2)}) collective-permute-start(f32[64,128]{1,0:T(8,128)S(1)} %get-tuple-element.76), channel_id=1, source_target_pairs={{0,1},{1,2},{2,3},{3,0},{4,5},{5,6},{6,7},{7,4},{8,9},{9,10},{10,1... | collective-permute-start | bytes 98312 | tf_op jit(solution)/shard_map/ppermute | solution.py:447
  4.9 1.5 %collective-permute-start.5 = (f32[64,128]{1,0:T(8,128)S(1)}, f32[64,128]{1,0:T(8,128)S(1)}, u32[]{:S(2)}, u32[]{:S(2)}) collective-permute-start(f32[64,128]{1,0:T(8,128)S(1)} %get-tuple-element.76), channel_id=1, source_target_pairs={{0,3},{1,0},{2,1},{3,2},{4,7},{5,4},{6,5},{7,6},{8,11},{9,8},{10,9... | collective-permute-start | bytes 98312 | tf_op jit(solution)/shard_map/ppermute | solution.py:447
  6.4 2.2 %collective-permute-start = (f32[128,128]{1,0:T(8,128)S(1)}, f32[128,128]{1,0:T(8,128)S(1)}, u32[]{:S(2)}, u32[]{:S(2)}) collective-permute-start(f32[128,128]{1,0:T(8,128)S(1)} %get-tuple-element.72), channel_id=1, source_target_pairs={{0,32},{32,64},{64,96},{96,128},{128,160},{160,192},{192,224},{224... | collective-permute-start | bytes 196616 | tf_op jit(solution)/shard_map/ppermute | solution.py:445
  8.6 0.6 collective-permute-start.1
  9.2 1.0 collective-permute-start.2
  10.2 0.0 collective-permute-done.4.zprev
  10.2 4.0 %collective-permute-start.3 = (f32[64,128]{1,0:T(8,128)S(1)}, f32[64,128]{1,0:T(8,128)S(1)}, u32[]{:S(2)}, u32[]{:S(2)}) collective-permute-start(f32[64,128]{1,0:T(8,128)S(1)} %get-tuple-element.75), channel_id=1, source_target_pairs={{0,28},{4,0},{8,4},{12,8},{16,12},{20,16},{24,20},{28,24},{1,29},{... | collective-permute-start | bytes 98312 | tf_op jit(solution)/shard_map/ppermute | solution.py:446
  14.2 0.7 bitcast_add_fusion
  15.0 0.8 index.1
  15.8 0.0 collective-permute-done.5.znext
  15.8 0.0 collective-permute-done.2.yprev
  15.8 0.0 collective-permute-done.3.ynext
  15.8 0.0 collective-permute-done.xprev
  15.8 0.0 collective-permute-done.1.xnext
  15.9 1.9 %curl.1 = (f32[6144,128]{1,0:T(8,128)S(1)}, f32[8,128]{1,0:T(8,128)S(1)}) custom-call(f32[6144,128]{1,0:T(8,128)S(1)} %get-tuple-element.71.vel, f32[128,128]{1,0:T(8,128)S(1)} %collective-permute-done.xprev, f32[128,128]{1,0:T(8,128)S(1)} %collective-permute-done.1.xnext, f32[64,128]{1,0:T(8,128)S(1)} %collective-permute-done.2.yprev, ...), custom_call_target="tpu_custom_call" | custom-call | flops 40000000 | bytes 7500000 | tf_op jit(solution)/shard_map/curl/pallas_call | solution.py:206
  17.7 0.2 collective-permute-start.6
  17.9 2.6 %collective-permute-start.7 = (f32[8,128]{1,0:T(8,128)S(1)}, f32[8,128]{1,0:T(8,128)S(1)}, u32[]{:S(2)}, u32[]{:S(2)}) collective-permute-start(f32[8,128]{1,0:T(8,128)S(1)} %get-tuple-element.120.one), channel_id=1, source_target_pairs={{0,2},{1,3},{2,0},{3,1},{4,6},{5,7},{6,4},{7,5},{8,10},{9,11},{10,... | collective-permute-start | bytes 12296 | tf_op jit(solution)/shard_map/ppermute | solution.py:451
  20.5 1.1 collective-permute-start.8
  21.6 0.0 copy-done.2
  21.6 1.5 %transform.1.coeffs = f32[6144,128]{1,0:T(8,128)S(1)} custom-call(f32[6144,128]{1,0:T(8,128)S(1)} %get-tuple-element.78.curls, bf16[2048,256]{1,0:T(8,128)(2,1)S(1)} %copy-done.2), custom_call_target="tpu_custom_call" | custom-call | flops 805306368 | bytes 7500000 | tf_op jit(solution)/shard_map/transform/pallas_call | solution.py:259
  23.1 0.0 collective-permute-done.6.two
  23.2 0.0 collective-permute-done.7.three
  23.2 0.0 collective-permute-done.8.four
  23.2 4.7 %pack45.1 = f32[8704,128]{1,0:T(8,128)S(1)} custom-call(s32[16,128]{1,0:T(8,128)S(1)} %get-tuple-element.70.words, f32[6144,128]{1,0:T(8,128)S(1)} %transform.1.coeffs, f32[64,128]{1,0:T(8,128)S(1)} %get-tuple-element.119.head, f32[8,128]{1,0:T(8,128)S(1)} %get-tuple-element.120.one, f32[8,128]{1,0:T(8,128)S(1)} %collective-permute-done.6.two, ...), custom_call_target="tpu_custom_call" | custom-call | flops 200000000 | bytes 8000000 | tf_op jit(solution)/shard_map/pack45/pallas_call | solution.py:315
  27.9 113.7 %all_to_all.9 = f32[64,136,128]{2,1,0:T(8,128)S(1)} all-to-all(f32[64,136,128]{2,1,0:T(8,128)S(1)} %bitcast.12), channel_id=1, replica_groups=mesh['gx'=8,'gy'=8,'wa'=4] {'gx','gy'}, dimensions={0} | all-to-all | bytes 8912896 | tf_op jit(solution)/shard_map/all_to_all | solution.py:428
  141.6 10.4 %unpack45.1 = (f32[3,4096,128]{2,1,0:T(8,128)}, s32[1,1]{1,0:T(1,128)}, f32[64,128]{1,0:T(8,128)S(1)}) custom-call(f32[8704,128]{1,0:T(8,128)S(1)} %bitcast.11), custom_call_target="tpu_custom_call" | custom-call | flops 200000000 | bytes 11000000 | tf_op jit(solution)/shard_map/unpack45/pallas_call | solution.py:398
  152.0 0.6 while.9
Async XLA Ops:
  0.0 1.9 %copy-start.1 = (f32[3,32,64,128]{3,2,1,0:T(8,128)S(1)}, f32[3,32,64,128]{3,2,1,0:T(8,128)}, u32[]{:S(2)}) copy-start(f32[3,32,64,128]{3,2,1,0:T(8,128)} %param.6) | copy-start | bytes 9437188
  1.9 19.7 %copy-start.2 = (bf16[2048,256]{1,0:T(8,128)(2,1)S(1)}, bf16[2048,256]{1,0:T(8,128)(2,1)}, u32[]{:S(2)}) copy-start(bf16[2048,256]{1,0:T(8,128)(2,1)} %constant.8.clone.tables) | copy-start | bytes 3145732
  2.7 7.5 %collective-permute-start.4 = (f32[64,128]{1,0:T(8,128)S(1)}, f32[64,128]{1,0:T(8,128)S(1)}, u32[]{:S(2)}, u32[]{:S(2)}) collective-permute-start(f32[64,128]{1,0:T(8,128)S(1)} %get-tuple-element.76), channel_id=1, source_target_pairs={{0,1},{1,2},{2,3},{3,0},{4,5},{5,6},{6,7},{7,4},{8,9},{9,10},{10,1... | collective-permute-start | bytes 98312 | tf_op jit(solution)/shard_map/ppermute | solution.py:447
  4.9 10.9 %collective-permute-start.5 = (f32[64,128]{1,0:T(8,128)S(1)}, f32[64,128]{1,0:T(8,128)S(1)}, u32[]{:S(2)}, u32[]{:S(2)}) collective-permute-start(f32[64,128]{1,0:T(8,128)S(1)} %get-tuple-element.76), channel_id=1, source_target_pairs={{0,3},{1,0},{2,1},{3,2},{4,7},{5,4},{6,5},{7,6},{8,11},{9,8},{10,9... | collective-permute-start | bytes 98312 | tf_op jit(solution)/shard_map/ppermute | solution.py:447
  6.4 9.4 %collective-permute-start = (f32[128,128]{1,0:T(8,128)S(1)}, f32[128,128]{1,0:T(8,128)S(1)}, u32[]{:S(2)}, u32[]{:S(2)}) collective-permute-start(f32[128,128]{1,0:T(8,128)S(1)} %get-tuple-element.72), channel_id=1, source_target_pairs={{0,32},{32,64},{64,96},{96,128},{128,160},{160,192},{192,224},{224... | collective-permute-start | bytes 196616 | tf_op jit(solution)/shard_map/ppermute | solution.py:445
  8.6 7.3 %collective-permute-start.1 = (f32[128,128]{1,0:T(8,128)S(1)}, f32[128,128]{1,0:T(8,128)S(1)}, u32[]{:S(2)}, u32[]{:S(2)}) collective-permute-start(f32[128,128]{1,0:T(8,128)S(1)} %get-tuple-element.73), channel_id=1, source_target_pairs={{0,224},{32,0},{64,32},{96,64},{128,96},{160,128},{192,160},{224,1... | collective-permute-start | bytes 196616 | tf_op jit(solution)/shard_map/ppermute | solution.py:445
  9.2 6.6 %collective-permute-start.2 = (f32[64,128]{1,0:T(8,128)S(1)}, f32[64,128]{1,0:T(8,128)S(1)}, u32[]{:S(2)}, u32[]{:S(2)}) collective-permute-start(f32[64,128]{1,0:T(8,128)S(1)} %get-tuple-element.74), channel_id=1, source_target_pairs={{0,4},{4,8},{8,12},{12,16},{16,20},{20,24},{24,28},{28,0},{1,5},{5... | collective-permute-start | bytes 98312 | tf_op jit(solution)/shard_map/ppermute | solution.py:446
  10.2 5.6 %collective-permute-start.3 = (f32[64,128]{1,0:T(8,128)S(1)}, f32[64,128]{1,0:T(8,128)S(1)}, u32[]{:S(2)}, u32[]{:S(2)}) collective-permute-start(f32[64,128]{1,0:T(8,128)S(1)} %get-tuple-element.75), channel_id=1, source_target_pairs={{0,28},{4,0},{8,4},{12,8},{16,12},{20,16},{24,20},{28,24},{1,29},{... | collective-permute-start | bytes 98312 | tf_op jit(solution)/shard_map/ppermute | solution.py:446
  17.7 5.4 %collective-permute-start.6 = (f32[8,128]{1,0:T(8,128)S(1)}, f32[8,128]{1,0:T(8,128)S(1)}, u32[]{:S(2)}, u32[]{:S(2)}) collective-permute-start(f32[8,128]{1,0:T(8,128)S(1)} %get-tuple-element.120.one), channel_id=1, source_target_pairs={{0,1},{1,2},{2,3},{3,0},{4,5},{5,6},{6,7},{7,4},{8,9},{9,10},{10,1... | collective-permute-start | bytes 12296 | tf_op jit(solution)/shard_map/ppermute | solution.py:451
  17.9 5.2 %collective-permute-start.7 = (f32[8,128]{1,0:T(8,128)S(1)}, f32[8,128]{1,0:T(8,128)S(1)}, u32[]{:S(2)}, u32[]{:S(2)}) collective-permute-start(f32[8,128]{1,0:T(8,128)S(1)} %get-tuple-element.120.one), channel_id=1, source_target_pairs={{0,2},{1,3},{2,0},{3,1},{4,6},{5,7},{6,4},{7,5},{8,10},{9,11},{10,... | collective-permute-start | bytes 12296 | tf_op jit(solution)/shard_map/ppermute | solution.py:451
  20.5 2.6 %collective-permute-start.8 = (f32[8,128]{1,0:T(8,128)S(1)}, f32[8,128]{1,0:T(8,128)S(1)}, u32[]{:S(2)}, u32[]{:S(2)}) collective-permute-start(f32[8,128]{1,0:T(8,128)S(1)} %get-tuple-element.120.one), channel_id=1, source_target_pairs={{0,3},{1,0},{2,1},{3,2},{4,7},{5,4},{6,5},{7,6},{8,11},{9,8},{10,9... | collective-permute-start | bytes 12296 | tf_op jit(solution)/shard_map/ppermute | solution.py:451
